TPU v7x, 32 devices: a whole 2x2x4 slice. The times are simulated.
32 devices in a mesh: dp: 32 (over z, y, x, core).
Axes of the slice: x: 2, y: 2, z: 4, core: 2. Of those that a mesh axis runs over, the one named last changes fastest.
Arguments:
- block_input: bfloat16 [8192, 3072], P('dp'), may hold values from -12 to 12
- segments: int32 [8192], P('dp'), may hold values from 0 to 8191, as said below
- cotangent: bfloat16 [8192, 3072], P('dp'), may hold values from -6 to 6
- gain_one: bfloat16 [3072], P('dp'), may hold values from 0.5 to 1.5
- w_z: bfloat16 [3072, 3072], P('dp'), may hold values from -0.109375 to 0.109375
- w_x: bfloat16 [3072, 3072], P('dp'), may hold values from -0.109375 to 0.109375
- w_bc: bfloat16 [3072, 512], P('dp'), may hold values from -0.109375 to 0.109375
- w_dt: bfloat16 [3072, 24], P('dp'), may hold values from -0.109375 to 0.109375
- conv_weight: bfloat16 [4, 3584], P(None, 'dp'), may hold values from -0.59765625 to 0.59765625
- conv_bias: bfloat16 [3584], P('dp'), may hold values from -3 to 3
- head_params: float32 [3, 24], replicated, may hold values from -3 to 1
- w_mout: bfloat16 [3072, 3072], P('dp'), may hold values from -0.109375 to 0.109375
- w_q: bfloat16 [3072, 1536], P('dp'), may hold values from -1 to 1
- w_kv: bfloat16 [3072, 512], P('dp'), may hold values from -1 to 1
- w_ao: bfloat16 [1536, 3072], P('dp'), may hold values from -0.4375 to 0.4375
- gain_two: bfloat16 [3072], P('dp'), may hold values from 0.5 to 1.5
- w_gate: bfloat16 [3072, 12288], P('dp'), may hold values from -0.109375 to 0.109375
- w_up: bfloat16 [3072, 12288], P('dp'), may hold values from -0.109375 to 0.109375
- w_down: bfloat16 [12288, 3072], P('dp'), may hold values from -0.0546875 to 0.0546875
Outputs:
- block_out: bfloat16 [8192, 3072], P('dp')
- grad_input: bfloat16 [8192, 3072], P('dp')
- grad_gain_one: float32 [3072], P('dp')
- grad_w_z: float32 [3072, 3072], P('dp')
- grad_w_x: float32 [3072, 3072], P('dp')
- grad_w_bc: float32 [3072, 512], P('dp')
- grad_w_dt: float32 [3072, 24], P('dp')
- grad_conv_weight: float32 [4, 3584], P(None, 'dp')
- grad_conv_bias: float32 [3584], P('dp')
- grad_head_params: float32 [3, 24], replicated
- grad_w_mout: float32 [3072, 3072], P('dp')
- grad_w_q: float32 [3072, 1536], P('dp')
- grad_w_kv: float32 [3072, 512], P('dp')
- grad_w_ao: float32 [1536, 3072], P('dp')
- grad_gain_two: float32 [3072], P('dp')
- grad_w_gate: float32 [3072, 12288], P('dp')
- grad_w_up: float32 [3072, 12288], P('dp')
- grad_w_down: float32 [12288, 3072], P('dp')
Inputs may be any that keep to these rules, and one draw needn't show every extreme that they name: `segments`: each token holds the global index of the first token of its sequence; a sequence lies within one aligned block of 256 tokens; in every draw some block is one sequence of 256 tokens, and the last token is a sequence of its own.
All inputs are finite; a program needn't handle non-finite values.
Results may differ from a plain program's by a relative error of at most 0.012.
Values may be sent and summed in bfloat16 or wider, within the bound.
A program may use at most 1.125 GiB of HBM per device.

v0:
```python
import jax
import jax.numpy as jnp
from jax import lax
from jax.sharding import PartitionSpec as P

HEADS = 24
HDIM = 128
NSTATE = 256
KCONV = 4
QHEADS = 12
KVHEADS = 2
DSSM = 3072


EPS = 1e-05
ROPE_BASE = 100000000000.0


def matmul(left, right):
    return jnp.dot(left, right, preferred_element_type=jnp.float32)


def mat_bt(left, right):
    return lax.dot_general(
        left, right, (((1,), (1,)), ((), ())), preferred_element_type=jnp.float32
    )


def mat_at(left, right):
    return lax.dot_general(
        left, right, (((0,), (0,)), ((), ())), preferred_element_type=jnp.float32
    )


def norm_forward(values, gain):
    rstd = lax.rsqrt(jnp.mean(values * values, axis=-1, keepdims=True) + EPS)
    normed = values * rstd
    return (normed, rstd, (normed * gain.astype(jnp.float32)).astype(jnp.bfloat16))


def norm_backward(grad_out, normed, rstd, gain):
    scaled = grad_out * gain.astype(jnp.float32)
    grad_in = rstd * (scaled - normed * jnp.mean(scaled * normed, axis=-1, keepdims=True))
    return (grad_in, jnp.sum(grad_out * normed, axis=0))


def rotate(values, position):
    half = values.shape[-1] // 2
    inverse = ROPE_BASE ** (-jnp.arange(half, dtype=jnp.float32) / half)
    angle = position.astype(jnp.float32)[:, None] * inverse[None, :]
    cosine = jnp.cos(angle)[:, None, :]
    sine = jnp.sin(angle)[:, None, :]
    first = values[..., :half]
    second = values[..., half:]
    return jnp.concatenate(
        [first * cosine - second * sine, second * cosine + first * sine], axis=-1
    )


def same_causal(segments):
    count = segments.shape[0]
    order = jnp.arange(count, dtype=jnp.int32)
    return (segments[:, None] == segments[None, :]) & (order[:, None] >= order[None, :])


def attention_core(q_part, kv_part, segments, position):
    count = q_part.shape[0]
    group = QHEADS // KVHEADS
    queries = rotate(q_part.reshape(count, QHEADS, HDIM), position).reshape(
        count, KVHEADS, group, HDIM
    )
    keys = rotate(kv_part[:, : KVHEADS * HDIM].reshape(count, KVHEADS, HDIM), position)
    values = kv_part[:, KVHEADS * HDIM :].reshape(count, KVHEADS, HDIM)
    scores = jnp.einsum(
        "tkgd,skd->kgts", queries, keys, precision=lax.Precision.HIGHEST
    ) * HDIM ** (-0.5)
    allowed = same_causal(segments)
    scores = jnp.where(allowed, scores, -1e30)
    top = jnp.max(scores, axis=-1, keepdims=True)
    weights = jnp.exp(scores - top)
    total = jnp.sum(weights, axis=-1, keepdims=True)
    mixed = jnp.einsum("kgts,skd->tkgd", weights / total, values, precision=lax.Precision.HIGHEST)
    return mixed.reshape(count, QHEADS * HDIM)


def mamba_core(z_part, x_part, bc_part, dt_part, conv_weight, conv_bias, head_params, segments):
    count = x_part.shape[0]
    mixed_in = jnp.concatenate([x_part, bc_part], axis=1)
    conv_acc = conv_bias[None, :] + conv_weight[0][None, :] * mixed_in
    for shift in range(1, KCONV):
        moved = jnp.concatenate(
            [jnp.zeros((shift, mixed_in.shape[1]), mixed_in.dtype), mixed_in[:-shift]], axis=0
        )
        linked = jnp.concatenate(
            [jnp.zeros((shift,), dtype=jnp.bool_), segments[shift:] == segments[:-shift]]
        )
        conv_acc = conv_acc + conv_weight[shift][None, :] * jnp.where(linked[:, None], moved, 0.0)
    conved = jax.nn.silu(conv_acc)
    x_conv = conved[:, :DSSM]
    b_conv = conved[:, DSSM : DSSM + NSTATE]
    c_conv = conved[:, DSSM + NSTATE :]
    step_size = jax.nn.softplus(dt_part + head_params[1][None, :])
    log_decay = -step_size * jnp.exp(head_params[0])[None, :]
    running = jnp.cumsum(log_decay, axis=0)
    allowed = same_causal(segments)[:, :, None]
    gap = jnp.where(allowed, running[:, None, :] - running[None, :, :], 0.0)
    inner = jnp.dot(c_conv, b_conv.T, precision=lax.Precision.HIGHEST)
    kernel = jnp.where(allowed, jnp.exp(gap), 0.0) * inner[:, :, None]
    heads_in = x_conv.reshape(count, HEADS, HDIM) * step_size[:, :, None]
    scanned = jnp.einsum("tsh,shp->thp", kernel, heads_in, precision=lax.Precision.HIGHEST)
    scanned = scanned + head_params[2][None, :, None] * x_conv.reshape(count, HEADS, HDIM)
    return scanned.reshape(count, DSSM) * jax.nn.silu(z_part)


def forward_pass(block_input, segments, position, weights, head_params):
    (
        gain_one,
        w_z,
        w_x,
        w_bc,
        w_dt,
        conv_weight,
        conv_bias,
        w_mout,
        w_q,
        w_kv,
        w_ao,
        gain_two,
        w_gate,
        w_up,
        w_down,
    ) = weights
    as_float = block_input.astype(jnp.float32)
    normed_one, rstd_one, normed_in = norm_forward(as_float, gain_one)
    z_part = matmul(normed_in, w_z)
    x_part = matmul(normed_in, w_x)
    bc_part = matmul(normed_in, w_bc)
    dt_part = matmul(normed_in, w_dt)
    q_part = matmul(normed_in, w_q)
    kv_part = matmul(normed_in, w_kv)
    mamba_y = mamba_core(
        z_part,
        x_part,
        bc_part,
        dt_part,
        conv_weight.astype(jnp.float32),
        conv_bias.astype(jnp.float32),
        head_params,
        segments,
    ).astype(jnp.bfloat16)
    attn_y = attention_core(q_part, kv_part, segments, position).astype(jnp.bfloat16)
    hidden = as_float + matmul(mamba_y, w_mout) + matmul(attn_y, w_ao)
    normed_two, rstd_two, normed_mid = norm_forward(hidden, gain_two)
    gate_pre = matmul(normed_mid, w_gate)
    up_pre = matmul(normed_mid, w_up)
    activated = (jax.nn.silu(gate_pre) * up_pre).astype(jnp.bfloat16)
    block_out = (hidden + matmul(activated, w_down)).astype(jnp.bfloat16)
    saved = (
        normed_one,
        rstd_one,
        normed_in,
        z_part,
        x_part,
        bc_part,
        dt_part,
        q_part,
        kv_part,
        mamba_y,
        attn_y,
        normed_two,
        rstd_two,
        normed_mid,
        gate_pre,
        up_pre,
        activated,
    )
    return (block_out, saved)


def backward_ffn(saved, cotangent, weights):
    (
        normed_one,
        rstd_one,
        normed_in,
        z_part,
        x_part,
        bc_part,
        dt_part,
        q_part,
        kv_part,
        mamba_y,
        attn_y,
        normed_two,
        rstd_two,
        normed_mid,
        gate_pre,
        up_pre,
        activated,
    ) = saved
    gain_two, w_gate, w_up, w_down = (weights[11], weights[12], weights[13], weights[14])
    grad_act = mat_bt(cotangent, w_down)
    grad_down = mat_at(activated, cotangent)
    sigma = jax.nn.sigmoid(gate_pre)
    grad_up_pre = (grad_act * gate_pre * sigma).astype(jnp.bfloat16)
    grad_gate_pre = (grad_act * up_pre * sigma * (1.0 + gate_pre * (1.0 - sigma))).astype(
        jnp.bfloat16
    )
    grad_mid = mat_bt(grad_gate_pre, w_gate) + mat_bt(grad_up_pre, w_up)
    grad_gate = mat_at(normed_mid, grad_gate_pre)
    grad_up = mat_at(normed_mid, grad_up_pre)
    grad_norm, grad_gain_two = norm_backward(grad_mid, normed_two, rstd_two, gain_two)
    grad_hidden = cotangent.astype(jnp.float32) + grad_norm
    return (grad_hidden, (grad_gain_two, grad_gate, grad_up, grad_down))


def backward_mixer(saved, grad_hidden, weights, head_params, segments, position):
    (
        normed_one,
        rstd_one,
        normed_in,
        z_part,
        x_part,
        bc_part,
        dt_part,
        q_part,
        kv_part,
        mamba_y,
        attn_y,
        normed_two,
        rstd_two,
        normed_mid,
        gate_pre,
        up_pre,
        activated,
    ) = saved
    gain_one, w_z, w_x, w_bc, w_dt, conv_weight, conv_bias, w_mout, w_q, w_kv, w_ao = weights[:11]
    grad_hidden_b = grad_hidden.astype(jnp.bfloat16)
    grad_attn = mat_bt(grad_hidden_b, w_ao)
    grad_ao = mat_at(attn_y, grad_hidden_b)
    grad_mamba = mat_bt(grad_hidden_b, w_mout)
    grad_mout = mat_at(mamba_y, grad_hidden_b)

    def attend(query_in, keyval_in):
        return attention_core(query_in, keyval_in, segments, position)

    _, attn_pull = jax.vjp(attend, q_part, kv_part)
    grad_q, grad_kv = attn_pull(grad_attn)

    def mixer(gate_in, inner_in, state_in, step_in, conv_in, bias_in, heads_in):
        return mamba_core(
            gate_in, inner_in, state_in, step_in, conv_in, bias_in, heads_in, segments
        )

    _, mamba_pull = jax.vjp(
        mixer,
        z_part,
        x_part,
        bc_part,
        dt_part,
        conv_weight.astype(jnp.float32),
        conv_bias.astype(jnp.float32),
        head_params,
    )
    grad_z, grad_x, grad_bc, grad_dt, grad_conv, grad_bias, grad_head = mamba_pull(grad_mamba)
    pieces = tuple(
        (
            piece.astype(jnp.bfloat16)
            for piece in (grad_z, grad_x, grad_bc, grad_dt, grad_q, grad_kv)
        )
    )
    matrices = (w_z, w_x, w_bc, w_dt, w_q, w_kv)
    grad_normed = mat_bt(pieces[0], matrices[0])
    for number in range(1, 6):
        grad_normed = grad_normed + mat_bt(pieces[number], matrices[number])
    weight_grads = tuple((mat_at(normed_in, piece) for piece in pieces))
    grad_norm, grad_gain_one = norm_backward(grad_normed, normed_one, rstd_one, gain_one)
    grad_input = (grad_hidden + grad_norm).astype(jnp.bfloat16)
    mixer_grads = (
        grad_gain_one,
        weight_grads[0],
        weight_grads[1],
        weight_grads[2],
        weight_grads[3],
        grad_conv,
        grad_bias,
        grad_mout,
        weight_grads[4],
        weight_grads[5],
        grad_ao,
    )
    return (grad_input, mixer_grads, grad_head)


def per_device(
    block_input,
    segments,
    cotangent,
    gain_one,
    w_z,
    w_x,
    w_bc,
    w_dt,
    conv_weight,
    conv_bias,
    head_params,
    w_mout,
    w_q,
    w_kv,
    w_ao,
    gain_two,
    w_gate,
    w_up,
    w_down,
):
    gathered = (
        lax.all_gather(gain_one, "dp", axis=0, tiled=True),
        lax.all_gather(w_z, "dp", axis=0, tiled=True),
        lax.all_gather(w_x, "dp", axis=0, tiled=True),
        lax.all_gather(w_bc, "dp", axis=0, tiled=True),
        lax.all_gather(w_dt, "dp", axis=0, tiled=True),
        lax.all_gather(conv_weight, "dp", axis=1, tiled=True),
        lax.all_gather(conv_bias, "dp", axis=0, tiled=True),
        lax.all_gather(w_mout, "dp", axis=0, tiled=True),
        lax.all_gather(w_q, "dp", axis=0, tiled=True),
        lax.all_gather(w_kv, "dp", axis=0, tiled=True),
        lax.all_gather(w_ao, "dp", axis=0, tiled=True),
        lax.all_gather(gain_two, "dp", axis=0, tiled=True),
        lax.all_gather(w_gate, "dp", axis=0, tiled=True),
        lax.all_gather(w_up, "dp", axis=0, tiled=True),
        lax.all_gather(w_down, "dp", axis=0, tiled=True),
    )
    count = block_input.shape[0]
    position = lax.axis_index("dp") * count + jnp.arange(count, dtype=jnp.int32) - segments
    block_out, saved = forward_pass(block_input, segments, position, gathered, head_params)
    again = (
        lax.all_gather(gain_one, "dp", axis=0, tiled=True),
        lax.all_gather(w_z, "dp", axis=0, tiled=True),
        lax.all_gather(w_x, "dp", axis=0, tiled=True),
        lax.all_gather(w_bc, "dp", axis=0, tiled=True),
        lax.all_gather(w_dt, "dp", axis=0, tiled=True),
        lax.all_gather(conv_weight, "dp", axis=1, tiled=True),
        lax.all_gather(conv_bias, "dp", axis=0, tiled=True),
        lax.all_gather(w_mout, "dp", axis=0, tiled=True),
        lax.all_gather(w_q, "dp", axis=0, tiled=True),
        lax.all_gather(w_kv, "dp", axis=0, tiled=True),
        lax.all_gather(w_ao, "dp", axis=0, tiled=True),
        lax.all_gather(gain_two, "dp", axis=0, tiled=True),
        lax.all_gather(w_gate, "dp", axis=0, tiled=True),
        lax.all_gather(w_up, "dp", axis=0, tiled=True),
        lax.all_gather(w_down, "dp", axis=0, tiled=True),
    )
    grad_hidden, ffn_grads = backward_ffn(saved, cotangent, again)
    grad_input, mixer_grads, grad_head = backward_mixer(
        saved, grad_hidden, again, head_params, segments, position
    )
    shares = (
        lax.psum_scatter(mixer_grads[0], "dp", scatter_dimension=0, tiled=True),
        lax.psum_scatter(mixer_grads[1], "dp", scatter_dimension=0, tiled=True),
        lax.psum_scatter(mixer_grads[2], "dp", scatter_dimension=0, tiled=True),
        lax.psum_scatter(mixer_grads[3], "dp", scatter_dimension=0, tiled=True),
        lax.psum_scatter(mixer_grads[4], "dp", scatter_dimension=0, tiled=True),
        lax.psum_scatter(mixer_grads[5], "dp", scatter_dimension=1, tiled=True),
        lax.psum_scatter(mixer_grads[6], "dp", scatter_dimension=0, tiled=True),
        lax.psum_scatter(mixer_grads[7], "dp", scatter_dimension=0, tiled=True),
        lax.psum_scatter(mixer_grads[8], "dp", scatter_dimension=0, tiled=True),
        lax.psum_scatter(mixer_grads[9], "dp", scatter_dimension=0, tiled=True),
        lax.psum_scatter(mixer_grads[10], "dp", scatter_dimension=0, tiled=True),
        lax.psum_scatter(ffn_grads[0], "dp", scatter_dimension=0, tiled=True),
        lax.psum_scatter(ffn_grads[1], "dp", scatter_dimension=0, tiled=True),
        lax.psum_scatter(ffn_grads[2], "dp", scatter_dimension=0, tiled=True),
        lax.psum_scatter(ffn_grads[3], "dp", scatter_dimension=0, tiled=True),
    )
    head_total = lax.psum(grad_head, "dp")
    return (
        block_out,
        grad_input,
        shares[0],
        shares[1],
        shares[2],
        shares[3],
        shares[4],
        shares[5],
        shares[6],
        head_total,
        shares[7],
        shares[8],
        shares[9],
        shares[10],
        shares[11],
        shares[12],
        shares[13],
        shares[14],
    )


def solution(mesh):
    in_specs = (
        P("dp", None),
        P("dp"),
        P("dp", None),
        P("dp"),
        P("dp", None),
        P("dp", None),
        P("dp", None),
        P("dp", None),
        P(None, "dp"),
        P("dp"),
        P(),
        P("dp", None),
        P("dp", None),
        P("dp", None),
        P("dp", None),
        P("dp"),
        P("dp", None),
        P("dp", None),
        P("dp", None),
    )
    out_specs = (
        P("dp", None),
        P("dp", None),
        P("dp"),
        P("dp", None),
        P("dp", None),
        P("dp", None),
        P("dp", None),
        P(None, "dp"),
        P("dp"),
        P(),
        P("dp", None),
        P("dp", None),
        P("dp", None),
        P("dp", None),
        P("dp"),
        P("dp", None),
        P("dp", None),
        P("dp", None),
    )
    return jax.shard_map(
        per_device, mesh=mesh, in_specs=in_specs, out_specs=out_specs, check_vma=False
    )
```

profile of v0, /device:TPU:0, one launch (start us, length us, event | category | flops | bytes accessed | tf_op | source)
XLA Modules:
  0.0 7831.1 jit_solution(8753187972918334531)
XLA Ops:
  14.9 42.4 all-reduce.31
  57.9 40.7 all-gather
  100.0 37.3 all-gather.1
  149.5 3.1 fusion.135
  152.6 64.3 all-gather.23.cloned.1.call-done
  216.9 6.7 fusion.128
  225.1 3.1 fusion.59
  232.5 67.2 all-gather.25.cloned.1.call-done
  299.7 8.0 fusion.146
  307.7 117.2 %all-gather.13.cloned.1.call-done = bf16[3072,3072]{1,0:T(8,128)(2,1)} async-done(((bf16[96,3072]{1,0:T(8,128)(2,1)}), bf16[3072,3072]{1,0:T(8,128)(2,1)}) %all-gather.13.cloned.1.call-update) | async-done | bytes 18874384 | tf_op jit(solution)/shard_map/all_gather | solution.py:318
  425.0 9.0 fusion.137
  438.2 6.0 fusion.27
  447.9 3.7 copy.210
  453.0 12.1 bitcast_add_fusion
  465.1 3.6 copy.194
  468.7 81.3 %all-gather.17.cloned.1.call-done = bf16[3072,3072]{1,0:T(8,128)(2,1)} async-done(((bf16[96,3072]{1,0:T(8,128)(2,1)}), bf16[3072,3072]{1,0:T(8,128)(2,1)}) %all-gather.17.cloned.1.call-update) | async-done | bytes 18874384 | tf_op jit(solution)/shard_map/all_gather | solution.py:317
  550.0 14.0 multiply_convert_fusion.4
  563.9 111.1 %all-gather.19.cloned.1.call-done = bf16[3072,3072]{1,0:T(8,128)(2,1)} async-done(((bf16[96,3072]{1,0:T(8,128)(2,1)}), bf16[3072,3072]{1,0:T(8,128)(2,1)}) %all-gather.19.cloned.1.call-update) | async-done | bytes 18874384 | tf_op jit(solution)/shard_map/all_gather | solution.py:323
  675.1 10.6 multiply_reduce_fusion.9
  687.8 384.3 %all-gather.27.cloned.1.call-done = bf16[3072,12288]{1,0:T(8,128)(2,1)} async-done(((bf16[96,12288]{1,0:T(8,128)(2,1)}), bf16[3072,12288]{1,0:T(8,128)(2,1)}) %all-gather.27.cloned.1.call-update) | async-done | bytes 75497488 | tf_op jit(solution)/shard_map/all_gather | solution.py:328
  1072.1 35.0 fusion.147
  1107.1 362.0 %all-gather.29.cloned.1.call-done = bf16[3072,12288]{1,0:T(8,128)(2,1)} async-done(((bf16[96,12288]{1,0:T(8,128)(2,1)}), bf16[3072,12288]{1,0:T(8,128)(2,1)}) %all-gather.29.cloned.1.call-update) | async-done | bytes 75497488 | tf_op jit(solution)/shard_map/all_gather | solution.py:329
  1469.1 35.1 fusion.148
  1504.2 361.7 %all-gather.31.cloned.1.call-done = bf16[12288,3072]{1,0:T(8,128)(2,1)} async-done(((bf16[384,3072]{1,0:T(8,128)(2,1)}), bf16[12288,3072]{1,0:T(8,128)(2,1)}) %all-gather.31.cloned.1.call-update) | async-done | bytes 75497488 | tf_op jit(solution)/shard_map/all_gather | solution.py:330
  1865.9 42.3 multiply_convert_fusion
  1908.3 31.7 fusion.149
  1940.0 32.5 multiply_reduce_fusion.4
  1972.5 4.6 fusion.119
  1977.1 14.3 multiply_reduce_fusion.5
  1994.5 12.5 fusion.18
  2009.9 7.9 fusion.44
  2020.7 4.6 fusion.69
  2025.3 3.5 multiply_reduce_fusion.7
  2035.6 3.6 copy.198
  2039.3 3.5 multiply_add_fusion.1
  2044.1 9.3 fusion.139
  2065.3 4.7 fusion.88
  2078.2 4.7 fusion.83
  2083.8 3.9 fusion.86
  2088.9 8.3 fusion.121
  2097.3 9.0 fusion.154
  2106.5 16.2 fusion.153
  2124.2 14.9 fusion.66
  2140.6 14.9 fusion.126
  2156.9 53.1 fusion.155
  2210.3 53.5 fusion.156
  2265.2 54.6 fusion.157
  2321.4 11.4 fusion.150
  2332.7 12.6 convolution_add_fusion.5
  2345.3 3.7 convolution_add_fusion.2
  2349.1 5.5 fusion.152
  2357.2 3.3 fusion.34
  2360.5 39.4 all-reduce.30
  2401.6 5.7 fusion.33
  2407.3 33.5 fusion.16
  2443.8 87.5 %reduce-scatter.21.cloned.1.call-done = f32[96,512]{1,0:T(8,128)} async-done(((f32[3072,512]{1,0:T(8,128)}), f32[96,512]{1,0:T(8,128)}) %reduce-scatter.21.cloned.1.call-update) | async-done | bytes 196624 | tf_op jit(solution)/shard_map/reduce_scatter | solution.py:360
  2531.2 212.7 %reduce-scatter.25.cloned.1.call-done = f32[96,1536]{1,0:T(8,128)} async-done(((f32[3072,1536]{1,0:T(8,128)}), f32[96,1536]{1,0:T(8,128)}) %reduce-scatter.25.cloned.1.call-update) | async-done | bytes 589840 | tf_op jit(solution)/shard_map/reduce_scatter | solution.py:365
  2743.9 213.0 %reduce-scatter.29.cloned.1.call-done = f32[48,3072]{1,0:T(8,128)} async-done(((f32[1536,3072]{1,0:T(8,128)}), f32[48,3072]{1,0:T(8,128)}) %reduce-scatter.29.cloned.1.call-update) | async-done | bytes 589840 | tf_op jit(solution)/shard_map/reduce_scatter | solution.py:367
  2956.9 355.0 %reduce-scatter.23.cloned.1.call-done = f32[96,3072]{1,0:T(8,128)} async-done(((f32[3072,3072]{1,0:T(8,128)}), f32[96,3072]{1,0:T(8,128)}) %reduce-scatter.23.cloned.1.call-update) | async-done | bytes 1179664 | tf_op jit(solution)/shard_map/reduce_scatter | solution.py:364
  3311.9 354.9 %reduce-scatter.19.cloned.1.call-done = f32[96,3072]{1,0:T(8,128)} async-done(((f32[3072,3072]{1,0:T(8,128)}), f32[96,3072]{1,0:T(8,128)}) %reduce-scatter.19.cloned.1.call-update) | async-done | bytes 1179664 | tf_op jit(solution)/shard_map/reduce_scatter | solution.py:359
  3666.9 355.2 %reduce-scatter.17.cloned.1.call-done = f32[96,3072]{1,0:T(8,128)} async-done(((f32[3072,3072]{1,0:T(8,128)}), f32[96,3072]{1,0:T(8,128)}) %reduce-scatter.17.cloned.1.call-update) | async-done | bytes 1179664 | tf_op jit(solution)/shard_map/reduce_scatter | solution.py:358
  4022.0 1266.9 %reduce-scatter.31.cloned.1.call-done = f32[96,12288]{1,0:T(8,128)} async-done(((f32[3072,12288]{1,0:T(8,128)}), f32[96,12288]{1,0:T(8,128)}) %reduce-scatter.31.cloned.1.call-update) | async-done | bytes 4718608 | tf_op jit(solution)/shard_map/reduce_scatter | solution.py:369
  5289.0 1266.8 %reduce-scatter.33.cloned.1.call-done = f32[96,12288]{1,0:T(8,128)} async-done(((f32[3072,12288]{1,0:T(8,128)}), f32[96,12288]{1,0:T(8,128)}) %reduce-scatter.33.cloned.1.call-update) | async-done | bytes 4718608 | tf_op jit(solution)/shard_map/reduce_scatter | solution.py:370
  6555.8 1268.1 %reduce-scatter.35.cloned.1.call-done = f32[384,3072]{1,0:T(8,128)} async-done(((f32[12288,3072]{1,0:T(8,128)}), f32[384,3072]{1,0:T(8,128)}) %reduce-scatter.35.cloned.1.call-update) | async-done | bytes 4718608 | tf_op jit(solution)/shard_map/reduce_scatter | solution.py:371
  (411 shorter events, 92.1 us)
Async XLA Ops:
  7.2 137.8 %all-gather.21.cloned.1.call-start = ((), (), s32[]{:S(2)}) async-start(), calls=%async_computation.16 | async-start | bytes 3244032 | tf_op jit(solution)/shard_map/all_gather | solution.py:325
  7.9 141.5 %all-gather.15.cloned.1.call-start = ((), (), s32[]{:S(2)}) async-start(), calls=%async_computation.13 | async-start | bytes 3244032 | tf_op jit(solution)/shard_map/all_gather | solution.py:319
  8.7 208.2 %all-gather.23.cloned.1.call-start = ((), (), s32[]{:S(2)}) async-start(), calls=%async_computation.17 | async-start | bytes 9732096 | tf_op jit(solution)/shard_map/all_gather | solution.py:324
  9.4 290.3 %all-gather.25.cloned.1.call-start = ((), (), s32[]{:S(2)}) async-start(), calls=%async_computation.18 | async-start | bytes 9732096 | tf_op jit(solution)/shard_map/all_gather | solution.py:326
  10.0 415.0 %all-gather.13.cloned.1.call-start = ((), (), s32[]{:S(2)}) async-start(), calls=%async_computation.12 | async-start | bytes 19464192 | tf_op jit(solution)/shard_map/all_gather | solution.py:318
  10.6 539.4 %all-gather.17.cloned.1.call-start = ((), (), s32[]{:S(2)}) async-start(), calls=%async_computation.14 | async-start | bytes 19464192 | tf_op jit(solution)/shard_map/all_gather | solution.py:317
  11.1 663.9 %all-gather.19.cloned.1.call-start = ((), (), s32[]{:S(2)}) async-start(), calls=%async_computation.15 | async-start | bytes 19464192 | tf_op jit(solution)/shard_map/all_gather | solution.py:323
  11.9 45.9 copy-start.116
  11.9 86.7 %copy-start.89 = (s32[256]{0:T(256)S(1)}, s32[256]{0:T(256)}, u32[]{:S(2)}) copy-start(s32[256]{0:T(256)} %param.20) | copy-start | bytes 3076
  11.9 88.1 %copy-start.103 = (bf16[96,24]{0,1:T(8,128)(2,1)S(1)}, bf16[96,24]{0,1:T(8,128)(2,1)}, u32[]{:S(2)}) copy-start(bf16[96,24]{0,1:T(8,128)(2,1)} %param.26) | copy-start | bytes 13828
  12.0 1060.2 %all-gather.27.cloned.1.call-start = ((), (), s32[]{:S(2)}) async-start(), calls=%async_computation.19 | async-start | bytes 77856768 | tf_op jit(solution)/shard_map/all_gather | solution.py:328
  12.7 124.9 %copy-start = (bf16[256,3072]{1,0:T(8,128)(2,1)S(1)}, bf16[256,3072]{1,0:T(8,128)(2,1)}, u32[]{:S(2)}) copy-start(bf16[256,3072]{1,0:T(8,128)(2,1)} %param.19) | copy-start | bytes 4718596
  12.7 1456.4 %all-gather.29.cloned.1.call-start = ((), (), s32[]{:S(2)}) async-start(), calls=%async_computation.20 | async-start | bytes 77856768 | tf_op jit(solution)/shard_map/all_gather | solution.py:329
  13.5 124.6 %copy-start.115 = (f32[3,24]{1,0:T(4,128)S(1)}, f32[3,24]{1,0:T(4,128)}, u32[]{:S(2)}) copy-start(f32[3,24]{1,0:T(4,128)} %param.29) | copy-start | bytes 868
  13.5 1852.4 %all-gather.31.cloned.1.call-start = ((), (), s32[]{:S(2)}) async-start(), calls=%async_computation.21 | async-start | bytes 77856768 | tf_op jit(solution)/shard_map/all_gather | solution.py:330
  14.1 2426.7 %reduce-scatter.39.cloned.1.call-start = ((), (), s32[]{:S(2)}) async-start(), calls=%async_computation.33 | async-start | bytes 1892352
  57.2 492.7 %copy-start.29 = (f32[3072]{0:T(1024)}, f32[3072]{0:T(1024)S(1)}, u32[]{:S(2)}) copy-start(f32[3072]{0:T(1024)S(1)} %convert_element_type.87) | copy-start | bytes 36868
  98.7 38.6 copy-start.118
  99.4 39.9 copy-start.120
  138.0 411.9 %copy-start.71 = (f32[256]{0:T(256)}, f32[256]{0:T(256)S(1)}, u32[]{:S(2)}) copy-start(f32[256]{0:T(256)S(1)} %add_rsqrt_fusion.1) | copy-start | bytes 3076
  138.0 9.9 copy-start.113
  140.5 7.5 copy-start.54
  140.5 83.1 %copy-start.52 = (f32[256,64]{0,1:T(8,128)}, f32[256,64]{0,1:T(8,128)S(1)}, u32[]{:S(2)}) copy-start(f32[256,64]{0,1:T(8,128)S(1)} %get-tuple-element.74) | copy-start | bytes 196612
  140.6 8.7 copy-start.47
  140.7 8.6 copy-start.49
  141.7 88.2 %copy-start.38 = (pred[256,256]{0,1:T(8,128)(4,1)}, pred[256,256]{0,1:T(8,128)(4,1)S(1)}, u32[]{:S(2)}) copy-start(pred[256,256]{0,1:T(8,128)(4,1)S(1)} %copy.158) | copy-start | bytes 196612
  149.4 74.5 copy-start.42
  149.4 74.5 copy-start.44
  152.5 282.6 %copy-start.23 = (f32[256,512]{1,0:T(8,128)}, f32[256,512]{1,0:T(8,128)S(1)}, u32[]{:S(2)}) copy-start(f32[256,512]{1,0:T(8,128)S(1)} %fusion.135) | copy-start | bytes 1572868
  232.5 75.2 copy-start.28
  435.1 9.1 copy-start.11
  453.0 12.1 copy-start.66
  675.1 12.3 copy-start.74
  687.8 781.3 %copy-start.16 = (bf16[256,3072]{1,0:T(8,128)(2,1)}, bf16[256,3072]{1,0:T(8,128)(2,1)S(1)}, u32[]{:S(2)}) copy-start(bf16[256,3072]{1,0:T(8,128)(2,1)S(1)} %multiply_convert_fusion.3) | copy-start | bytes 4718596
  1107.1 758.8 %copy-start.18 = (bf16[256,3072]{1,0:T(8,128)(2,1)S(1)}, bf16[256,3072]{1,0:T(8,128)(2,1)}, u32[]{:S(2)}) copy-start(bf16[256,3072]{1,0:T(8,128)(2,1)} %param.21) | copy-start | bytes 4718596
  1908.3 31.7 copy-start.14
  1908.3 31.7 copy-start.75
  1908.3 31.7 copy-start.97
  1994.4 15.4 copy-start.34
  1994.4 15.4 copy-start.35
  1994.5 23.3 slice-start
  1994.5 23.3 slice-start.1
  2009.9 7.9 slice-start.2
  2009.9 7.9 copy-start.20
  2053.4 7.0 copy-start.1
  2053.4 7.0 copy-start.30
  2053.5 7.0 copy-start.72
  2055.5 386.8 %reduce-scatter.37.cloned.1.call-start = ((), (), s32[]{:S(2)}) async-start(), calls=%async_computation.32 | async-start | bytes 1622016
  2060.4 9.6 copy-start.85
  2065.3 378.5 %reduce-scatter.27.cloned.1.call-start = ((), (), s32[]{:S(2)}) async-start(), calls=%async_computation.27 | async-start | bytes 6488064 | tf_op jit(solution)/shard_map/reduce_scatter | solution.py:366
  2070.1 461.1 %reduce-scatter.21.cloned.1.call-start = ((), (), s32[]{:S(2)}) async-start(), calls=%async_computation.24 | async-start | bytes 6488064 | tf_op jit(solution)/shard_map/reduce_scatter | solution.py:360
  2082.9 661.0 %reduce-scatter.25.cloned.1.call-start = ((), (), s32[]{:S(2)}) async-start(), calls=%async_computation.26 | async-start | bytes 19464192 | tf_op jit(solution)/shard_map/reduce_scatter | solution.py:365
  2097.2 859.7 %reduce-scatter.29.cloned.1.call-start = ((), (), s32[]{:S(2)}) async-start(), calls=%async_computation.28 | async-start | bytes 19464192 | tf_op jit(solution)/shard_map/reduce_scatter | solution.py:367
  2106.3 1205.7 %reduce-scatter.23.cloned.1.call-start = ((), (), s32[]{:S(2)}) async-start(), calls=%async_computation.25 | async-start | bytes 38928384 | tf_op jit(solution)/shard_map/reduce_scatter | solution.py:364
  2122.8 1544.1 %reduce-scatter.19.cloned.1.call-start = ((), (), s32[]{:S(2)}) async-start(), calls=%async_computation.23 | async-start | bytes 38928384 | tf_op jit(solution)/shard_map/reduce_scatter | solution.py:359
  2139.2 1882.8 %reduce-scatter.17.cloned.1.call-start = ((), (), s32[]{:S(2)}) async-start(), calls=%async_computation.22 | async-start | bytes 38928384 | tf_op jit(solution)/shard_map/reduce_scatter | solution.py:358
  2155.5 3133.4 %reduce-scatter.31.cloned.1.call-start = ((), (), s32[]{:S(2)}) async-start(), calls=%async_computation.29 | async-start | bytes 155713536 | tf_op jit(solution)/shard_map/reduce_scatter | solution.py:369
  2210.0 4345.8 %reduce-scatter.33.cloned.1.call-start = ((), (), s32[]{:S(2)}) async-start(), calls=%async_computation.30 | async-start | bytes 155713536 | tf_op jit(solution)/shard_map/reduce_scatter | solution.py:370
  2263.9 5560.0 %reduce-scatter.35.cloned.1.call-start = ((), (), s32[]{:S(2)}) async-start(), calls=%async_computation.31 | async-start | bytes 155713536 | tf_op jit(solution)/shard_map/reduce_scatter | solution.py:371
  2321.3 11.4 copy-start.27
  2332.7 12.6 copy-start.37
  2357.1 44.5 copy-start.76
  2357.1 44.5 copy-start.98
  2357.1 44.5 copy-start.102
  (88 other events, 261.0 us)
Sparse Core Ops, SparseCore 0:
  10.9 61.8 all-gather.20
  75.6 58.4 all-gather.14
  137.1 79.7 all-gather.22
  219.6 80.0 all-gather.24
  302.5 122.4 all-gather.12
  427.7 122.1 all-gather.16
  552.9 122.1 all-gather.18
  678.0 394.0 all-gather.26
  1075.0 394.0 all-gather.28
  1471.8 394.0 all-gather.30
  2055.6 136.1 reduce-scatter.38
  2196.9 93.7 reduce-scatter.36
  2297.0 114.2 reduce-scatter.26
  2417.3 113.8 reduce-scatter.20
  2538.0 205.8 reduce-scatter.24
  2750.8 206.1 reduce-scatter.28
  2963.8 348.1 reduce-scatter.22
  3318.8 348.0 reduce-scatter.18
  3673.8 348.1 reduce-scatter.16
  4028.9 1260.0 reduce-scatter.30
  5296.0 1259.7 reduce-scatter.32
  6562.8 1261.0 reduce-scatter.34
where the time goes:
time: 7840 us; the launch traced here: 7830 us
  waiting for transfers between devices  6940 us (89%)
  matrix products  613 us (8%)
  blocking collectives  160 us (2%)
    reduce_scatter x1, waiting for transfers between devices, per_device(): lax.psum_scatter(ffn_grads[3], 'dp', scatter_dimension=0, tiled=True)  1270 us
    reduce_scatter x1, waiting for transfers between devices, per_device(): lax.psum_scatter(ffn_grads[1], 'dp', scatter_dimension=0, tiled=True)  1270 us
    reduce_scatter x1, waiting for transfers between devices, per_device(): lax.psum_scatter(ffn_grads[2], 'dp', scatter_dimension=0, tiled=True)  1270 us
    all_gather x1, waiting for transfers between devices, per_device(): lax.all_gather(w_gate, 'dp', axis=0, tiled=True)  384 us
    all_gather x1, waiting for transfers between devices, per_device(): lax.all_gather(w_up, 'dp', axis=0, tiled=True)  362 us
    all_gather x1, waiting for transfers between devices, per_device(): lax.all_gather(w_down, 'dp', axis=0, tiled=True)  362 us
    reduce_scatter x1, waiting for transfers between devices, per_device(): lax.psum_scatter(mixer_grads[1], 'dp', scatter_dimension=0, tiled=True)  355 us
    reduce_scatter x1, waiting for transfers between devices, per_device(): lax.psum_scatter(mixer_grads[7], 'dp', scatter_dimension=0, tiled=True)  355 us
  transfers between devices with their start and end apart: 22, of which 17 were waited for; matrix products, arithmetic and copies ran while one was open for 7% of the time, Pallas kernels for 0%

commit v1 on v0

v1 whole, which is shorter than its diff:
```python
import functools

import jax
import jax.numpy as jnp
from jax import lax
from jax.experimental import pallas as pl
from jax.experimental.pallas import tpu as pltpu
from jax.sharding import PartitionSpec as P

HEADS = 24
HDIM = 128
NSTATE = 256
KCONV = 4
QHEADS = 12
KVHEADS = 2
DSSM = 3072


EPS = 1e-05
ROPE_BASE = 100000000000.0


def matmul(left, right):
    return jnp.dot(left, right, preferred_element_type=jnp.float32)


def mat_bt(left, right):
    return lax.dot_general(
        left, right, (((1,), (1,)), ((), ())), preferred_element_type=jnp.float32
    )


def mat_at(left, right):
    return lax.dot_general(
        left, right, (((0,), (0,)), ((), ())), preferred_element_type=jnp.float32
    )


def norm_forward(values, gain):
    rstd = lax.rsqrt(jnp.mean(values * values, axis=-1, keepdims=True) + EPS)
    normed = values * rstd
    return (normed, rstd, (normed * gain.astype(jnp.float32)).astype(jnp.bfloat16))


def norm_backward(grad_out, normed, rstd, gain):
    scaled = grad_out * gain.astype(jnp.float32)
    grad_in = rstd * (scaled - normed * jnp.mean(scaled * normed, axis=-1, keepdims=True))
    return (grad_in, jnp.sum(grad_out * normed, axis=0))


def rotate(values, position):
    half = values.shape[-1] // 2
    inverse = ROPE_BASE ** (-jnp.arange(half, dtype=jnp.float32) / half)
    angle = position.astype(jnp.float32)[:, None] * inverse[None, :]
    cosine = jnp.cos(angle)[:, None, :]
    sine = jnp.sin(angle)[:, None, :]
    first = values[..., :half]
    second = values[..., half:]
    return jnp.concatenate(
        [first * cosine - second * sine, second * cosine + first * sine], axis=-1
    )


def same_causal(segments):
    count = segments.shape[0]
    order = jnp.arange(count, dtype=jnp.int32)
    return (segments[:, None] == segments[None, :]) & (order[:, None] >= order[None, :])


def attention_core(q_part, kv_part, segments, position):
    count = q_part.shape[0]
    group = QHEADS // KVHEADS
    queries = rotate(q_part.reshape(count, QHEADS, HDIM), position).reshape(
        count, KVHEADS, group, HDIM
    )
    keys = rotate(kv_part[:, : KVHEADS * HDIM].reshape(count, KVHEADS, HDIM), position)
    values = kv_part[:, KVHEADS * HDIM :].reshape(count, KVHEADS, HDIM)
    scores = jnp.einsum(
        "tkgd,skd->kgts", queries, keys, precision=lax.Precision.HIGHEST
    ) * HDIM ** (-0.5)
    allowed = same_causal(segments)
    scores = jnp.where(allowed, scores, -1e30)
    top = jnp.max(scores, axis=-1, keepdims=True)
    weights = jnp.exp(scores - top)
    total = jnp.sum(weights, axis=-1, keepdims=True)
    mixed = jnp.einsum("kgts,skd->tkgd", weights / total, values, precision=lax.Precision.HIGHEST)
    return mixed.reshape(count, QHEADS * HDIM)


def mamba_core(z_part, x_part, bc_part, dt_part, conv_weight, conv_bias, head_params, segments):
    count = x_part.shape[0]
    mixed_in = jnp.concatenate([x_part, bc_part], axis=1)
    conv_acc = conv_bias[None, :] + conv_weight[0][None, :] * mixed_in
    for shift in range(1, KCONV):
        moved = jnp.concatenate(
            [jnp.zeros((shift, mixed_in.shape[1]), mixed_in.dtype), mixed_in[:-shift]], axis=0
        )
        linked = jnp.concatenate(
            [jnp.zeros((shift,), dtype=jnp.bool_), segments[shift:] == segments[:-shift]]
        )
        conv_acc = conv_acc + conv_weight[shift][None, :] * jnp.where(linked[:, None], moved, 0.0)
    conved = jax.nn.silu(conv_acc)
    x_conv = conved[:, :DSSM]
    b_conv = conved[:, DSSM : DSSM + NSTATE]
    c_conv = conved[:, DSSM + NSTATE :]
    step_size = jax.nn.softplus(dt_part + head_params[1][None, :])
    log_decay = -step_size * jnp.exp(head_params[0])[None, :]
    running = jnp.cumsum(log_decay, axis=0)
    allowed = same_causal(segments)[:, :, None]
    gap = jnp.where(allowed, running[:, None, :] - running[None, :, :], 0.0)
    inner = jnp.dot(c_conv, b_conv.T, precision=lax.Precision.HIGHEST)
    kernel = jnp.where(allowed, jnp.exp(gap), 0.0) * inner[:, :, None]
    heads_in = x_conv.reshape(count, HEADS, HDIM) * step_size[:, :, None]
    scanned = jnp.einsum("tsh,shp->thp", kernel, heads_in, precision=lax.Precision.HIGHEST)
    scanned = scanned + head_params[2][None, :, None] * x_conv.reshape(count, HEADS, HDIM)
    return scanned.reshape(count, DSSM) * jax.nn.silu(z_part)


VMEM_LIMIT = 66000000


class Torus:
    def __init__(self, mesh):
        spots = [device.coords for device in mesh.devices.flat]
        nx, ny, nz = (max(s[a] for s in spots) - min(s[a] for s in spots) + 1 for a in range(3))
        assert nx * ny * nz * 2 == mesh.shape["dp"]
        self.n = mesh.shape["dp"]
        self.nz = nz
        self.plane = 2 * nx * ny
        self.same = nx == ny
        self.n2, self.n3 = ny, nx
        self.far, self.near = 2 * nx, 2

    def order(self):
        return [
            (k, i, j) for k in range(self.nz) for i in range(self.n2) for j in range(self.n3)
        ]


def flip(value, step):
    out, bit = value, 1
    while bit <= step:
        if step & bit:
            out = out + bit - 2 * bit * ((value // bit) % 2)
        bit *= 2
    return out


class Place:
    def __init__(self, torus):
        me = lax.axis_index("dp")
        self.me, self.core = me, me % 2
        self.z = me // torus.plane
        far = (me // torus.far) % torus.n2
        near = (me // torus.near) % torus.n3
        if torus.same:
            self.second = far + self.core * (near - far)
            self.third = near + self.core * (far - near)
            self.step2 = torus.far + self.core * (torus.near - torus.far)
            self.step3 = torus.near + self.core * (torus.far - torus.near)
        else:
            self.second, self.third = far, near
            self.step2, self.step3 = torus.far, torus.near
        self.torus = torus
        self.sibling = me + 1 - 2 * self.core

    def at(self, k, i, j):
        return (
            flip(self.z, k) * self.torus.plane
            + flip(self.second, i) * self.step2
            + flip(self.third, j) * self.step3
            + self.core
        )

    def peers(self):
        t = self.torus
        return (
            [self.at(k, 0, 0) for k in range(1, t.nz)]
            + [self.at(0, i, 0) for i in range(1, t.n2)]
            + [self.at(0, 0, j) for j in range(1, t.n3)]
            + [self.sibling]
        )


def greet(place):
    barrier = pltpu.get_barrier_semaphore()
    peers = place.peers()
    for peer in peers:
        pl.semaphore_signal(
            barrier, inc=1, device_id=(peer,), device_id_type=pl.DeviceIdType.MESH
        )
    pl.semaphore_wait(barrier, len(peers))


def remote(src, dst, send, recv, device):
    return pltpu.make_async_remote_copy(
        src_ref=src,
        dst_ref=dst,
        send_sem=send,
        recv_sem=recv,
        device_id=(device,),
        device_id_type=pl.DeviceIdType.MESH,
    )


def spread(torus, place, ins, outs, send_sem, recv_sem, local_sem):
    count = len(ins)
    started = []

    def push(block, device, own=False):
        for a in range(count):
            source = ins[a] if own else outs[a].at[block]
            copy = remote(
                source,
                outs[a].at[block],
                send_sem.at[a, len(started) // count],
                recv_sem.at[a, block],
                device,
            )
            copy.start()
            started.append(copy)

    def arrive(block):
        for a in range(count):
            remote(
                outs[a].at[block],
                outs[a].at[block],
                send_sem.at[a, 0],
                recv_sem.at[a, block],
                place.sibling,
            ).wait_recv()

    own_copies = [
        pltpu.make_async_copy(ins[a], outs[a].at[place.me], local_sem.at[a])
        for a in range(count)
    ]
    for copy in own_copies:
        copy.start()
    for k, i, j in torus.order():
        block = place.at(k, i, j)
        own = (k, i, j) == (0, 0, 0)
        if not own:
            arrive(block)
        if own:
            for step in range(1, torus.nz):
                push(block, place.at(step, 0, 0), own)
        if i == 0 and j == 0:
            for step in range(1, torus.n2):
                push(block, place.at(0, step, 0), own)
        if j == 0:
            for step in range(1, torus.n3):
                push(block, place.at(0, 0, step), own)
        push(block, place.sibling, own)
    for copy in own_copies:
        copy.wait()
    for k, i, j in torus.order():
        block = other(place, k, i, j)
        arrive(block)
    for copy in started:
        copy.wait_send()


def other(place, k, i, j):
    t = place.torus
    if t.same:
        return (
            flip(place.z, k) * t.plane
            + flip(place.third, i) * place.step3
            + flip(place.second, j) * place.step2
            + (1 - place.core)
        )
    return (
        flip(place.z, k) * t.plane
        + flip(place.second, i) * place.step2
        + flip(place.third, j) * place.step3
        + (1 - place.core)
    )


def sends_of(torus):
    nz, n2, n3 = torus.nz, torus.n2, torus.n3
    return (nz - 1) + nz * (n2 - 1) + nz * n2 * (n3 - 1) + nz * n2 * n3


def gather_kernel(torus, count, *refs):
    ins, outs = refs[:count], refs[count : 2 * count]
    send_sem, recv_sem, local_sem = refs[2 * count :]
    place = Place(torus)
    greet(place)
    spread(torus, place, ins, outs, send_sem, recv_sem, local_sem)


def gather(torus, arrays, name, ident):
    count, n = len(arrays), torus.n
    return pl.pallas_call(
        functools.partial(gather_kernel, torus, count),
        out_shape=[jax.ShapeDtypeStruct((n,) + a.shape, a.dtype) for a in arrays],
        in_specs=[pl.BlockSpec(memory_space=pltpu.VMEM)] * count,
        out_specs=[pl.BlockSpec(memory_space=pl.ANY)] * count,
        scratch_shapes=[
            pltpu.SemaphoreType.DMA((count, sends_of(torus))),
            pltpu.SemaphoreType.DMA((count, n)),
            pltpu.SemaphoreType.DMA((count,)),
        ],
        compiler_params=pltpu.CompilerParams(
            collective_id=ident, has_side_effects=True, vmem_limit_bytes=VMEM_LIMIT
        ),
        name=name,
    )(*arrays)


def scatter_kernel(torus, first, wide, part_ref, out_ref, stage, from_core, from_third, from_second,
                   from_z, load_sem, core_sem, third_sem, second_sem, z_sem, send_sem):
    place = Place(torus)
    greet(place)
    nz, n2, n3 = torus.nz, torus.n2, torus.n3
    order = [(k, i, j) for k in reversed(range(nz)) for i in reversed(range(n2)) for j in reversed(range(n3))]
    columns = pl.ds(first, wide)
    started = []

    def slot_of(k, i, j):
        return (k * n2 + i) * n3 + j

    def send(src, dst, sem, device):
        copy = remote(src, dst, send_sem.at[len(started)], sem, device)
        copy.start()
        started.append(copy)

    def receive(dst, sem):
        remote(dst, dst, send_sem.at[0], sem, place.sibling).wait_recv()

    for k, i, j in order:
        s = slot_of(k, i, j)
        send(part_ref.at[other(place, k, i, j), :, columns], from_core.at[s], core_sem.at[s], place.sibling)

    def load(number):
        k, i, j = order[number]
        return pltpu.make_async_copy(
            part_ref.at[place.at(k, i, j), :, columns], stage.at[number % 2], load_sem.at[number % 2]
        )

    load(0).start()
    for number, (k, i, j) in enumerate(order):
        s = slot_of(k, i, j)
        if number + 1 < len(order):
            load(number + 1).start()
        load(number).wait()
        receive(from_core.at[s], core_sem.at[s])
        add(from_core.at[s], stage.at[number % 2])
        if j:
            t = (k * n2 + i) * (n3 - 1) + j - 1
            send(from_core.at[s], from_third.at[t], third_sem.at[t], place.at(0, 0, j))
    for k in reversed(range(nz)):
        for i in reversed(range(n2)):
            s = slot_of(k, i, 0)
            for j in range(1, n3):
                t = (k * n2 + i) * (n3 - 1) + j - 1
                receive(from_third.at[t], third_sem.at[t])
                add(from_core.at[s], from_third.at[t])
            if i:
                t = k * (n2 - 1) + i - 1
                send(from_core.at[s], from_second.at[t], second_sem.at[t], place.at(0, i, 0))
        s = slot_of(k, 0, 0)
        for i in range(1, n2):
            t = k * (n2 - 1) + i - 1
            receive(from_second.at[t], second_sem.at[t])
            add(from_core.at[s], from_second.at[t])
        if k:
            send(from_core.at[s], from_z.at[k - 1], z_sem.at[k - 1], place.at(k, 0, 0))
    for k in range(1, nz):
        receive(from_z.at[k - 1], z_sem.at[k - 1])
        add(from_core.at[0], from_z.at[k - 1])
    out_ref[...] = from_core[0]
    for copy in started:
        copy.wait_send()


def add(into, term):
    rows = into.shape[0]
    step = 16
    if rows % step:
        into[...] = (into[...].astype(jnp.float32) + term[...].astype(jnp.float32)).astype(into.dtype)
        return

    @pl.loop(0, rows // step)
    def _(index):
        piece = pl.ds(pl.multiple_of(index * step, step), step)
        into[piece, :] = (
            into[piece, :].astype(jnp.float32) + term[piece, :].astype(jnp.float32)
        ).astype(into.dtype)


def scatter(torus, part, name, ident):
    n, rows, width = part.shape
    nz, n2, n3 = torus.nz, torus.n2, torus.n3
    thirds, seconds = nz * n2 * (n3 - 1), nz * (n2 - 1)
    blocks = nz * n2 * n3 + thirds + seconds + nz - 1 + 3
    lanes = -(-width // 128)
    tile = (-(-rows // 16) * 16) * 128 * part.dtype.itemsize
    pieces = 1
    while blocks * tile * -(-lanes // pieces) > VMEM_LIMIT - 6 * 2**20:
        pieces += 1
    wide = -(-lanes // pieces) * 128
    outs = []
    for number, first in enumerate(range(0, width, wide)):
        size = min(wide, width - first)
        block = (rows, size)
        sends = nz * n2 * n3 + thirds + seconds + nz - 1
        outs.append(
            pl.pallas_call(
                functools.partial(scatter_kernel, torus, first, size),
                out_shape=jax.ShapeDtypeStruct(block, part.dtype),
                in_specs=[pl.BlockSpec(memory_space=pl.ANY)],
                out_specs=pl.BlockSpec(memory_space=pltpu.VMEM),
                scratch_shapes=[
                    pltpu.VMEM((2,) + block, part.dtype),
                    pltpu.VMEM((nz * n2 * n3,) + block, part.dtype),
                    pltpu.VMEM((thirds,) + block, part.dtype),
                    pltpu.VMEM((seconds,) + block, part.dtype),
                    pltpu.VMEM((nz - 1,) + block, part.dtype),
                    pltpu.SemaphoreType.DMA((2,)),
                    pltpu.SemaphoreType.DMA((nz * n2 * n3,)),
                    pltpu.SemaphoreType.DMA((thirds,)),
                    pltpu.SemaphoreType.DMA((seconds,)),
                    pltpu.SemaphoreType.DMA((nz - 1,)),
                    pltpu.SemaphoreType.DMA((sends,)),
                ],
                compiler_params=pltpu.CompilerParams(
                    collective_id=ident + number, has_side_effects=True, vmem_limit_bytes=VMEM_LIMIT
                ),
                name=f"{name}_{number}",
            )(part)
        )
    return outs[0] if len(outs) == 1 else jnp.concatenate(outs, axis=1)


def pack_small(parts):
    return jnp.concatenate([part.reshape(-1) for part in parts])


def weave(wide, narrow, ways):
    count = wide.shape[0]
    return jnp.concatenate(
        [wide.reshape(count, ways, -1), narrow.reshape(count, ways, -1)], axis=2
    ).reshape(count, -1)


def per_device(
    torus,
    block_input,
    segments,
    cotangent,
    gain_one,
    w_z,
    w_x,
    w_bc,
    w_dt,
    conv_weight,
    conv_bias,
    head_params,
    w_mout,
    w_q,
    w_kv,
    w_ao,
    gain_two,
    w_gate,
    w_up,
    w_down,
):
    ways = torus.n
    count, width = block_input.shape
    rows = w_z.shape[0]
    position = lax.axis_index("dp") * count + jnp.arange(count, dtype=jnp.int32) - segments
    f32, bf16 = jnp.float32, jnp.bfloat16

    smalls = (gain_one, gain_two, conv_bias, conv_weight.T)
    packed = pack_small(smalls)
    extra = -(-packed.size // rows)
    packed = jnp.pad(packed, (0, extra * rows - packed.size)).reshape(rows, extra)
    projections = (w_z, w_x, w_bc, w_q, w_kv, w_dt)
    edges = [0]
    for w in projections:
        edges.append(edges[-1] + w.shape[1])
    share_in = jnp.concatenate(projections + (packed,), axis=1)
    share_out = jnp.concatenate([w_mout, w_ao], axis=0)
    all_in, all_out = gather(torus, [share_in, share_out], "spread_weights", 1)
    packed_all = all_in[:, :, edges[-1] :].reshape(ways, -1)
    w_in = all_in.reshape(ways * rows, -1)
    w_out = all_out.reshape(-1, width)
    cut = 0
    small_all = []
    for part in smalls:
        piece = packed_all[:, cut : cut + part.size]
        small_all.append(piece.reshape((ways * part.shape[0],) + part.shape[1:]))
        cut += part.size
    gain_one_all, gain_two_all, bias_all, conv_all = small_all
    conv_all = conv_all.T.astype(f32)
    bias_all = bias_all.astype(f32)

    as_float = block_input.astype(f32)
    normed_one, rstd_one, normed_in = norm_forward(as_float, gain_one_all)
    joint = matmul(normed_in, w_in)
    z_part, x_part, bc_part, q_part, kv_part, dt_part = (
        joint[:, edges[k] : edges[k + 1]] for k in range(6)
    )

    def mixer(gate_in, inner_in, state_in, step_in, conv_in, bias_in, heads_in):
        return mamba_core(
            gate_in, inner_in, state_in, step_in, conv_in, bias_in, heads_in, segments
        )

    def attend(query_in, keyval_in):
        return attention_core(query_in, keyval_in, segments, position)

    mamba_out, mamba_pull = jax.vjp(
        mixer, z_part, x_part, bc_part, dt_part, conv_all, bias_all, head_params
    )
    attn_out, attn_pull = jax.vjp(attend, q_part, kv_part)
    mixed = weave(mamba_out.astype(bf16), attn_out.astype(bf16), ways)
    hidden = as_float + matmul(mixed, w_out)
    normed_two, rstd_two, normed_mid = norm_forward(hidden, gain_two_all)

    w_gate_own = lax.all_to_all(w_gate, "dp", split_axis=1, concat_axis=0, tiled=True)
    w_up_own = lax.all_to_all(w_up, "dp", split_axis=1, concat_axis=0, tiled=True)
    cot_all = gather(torus, [cotangent], "spread_cotangent", 2)[0].reshape(-1, width)
    mid_all = gather(torus, [normed_mid], "spread_mid", 3)[0].reshape(-1, width)
    gate_pre = matmul(mid_all, w_gate_own)
    up_pre = matmul(mid_all, w_up_own)
    sigma = jax.nn.sigmoid(gate_pre)
    activated = (gate_pre * sigma * up_pre).astype(bf16)
    grad_act = mat_bt(cot_all, w_down)
    grad_up_pre = (grad_act * gate_pre * sigma).astype(bf16)
    grad_gate_pre = (grad_act * up_pre * sigma * (1.0 + gate_pre * (1.0 - sigma))).astype(bf16)
    mid_share = (mat_bt(grad_gate_pre, w_gate_own) + mat_bt(grad_up_pre, w_up_own)).astype(bf16)
    out_share = matmul(activated, w_down).astype(bf16)
    blocks = (ways, count, width)
    grad_mid = scatter(torus, mid_share.reshape(blocks), "fold_mid", 16).astype(f32)
    out_sum = scatter(torus, out_share.reshape(blocks), "fold_out", 32)
    block_out = (hidden + out_sum.astype(f32)).astype(bf16)
    grad_w_down = mat_at(activated, cot_all)
    grad_w_gate = lax.all_to_all(
        mat_at(mid_all, grad_gate_pre).astype(bf16), "dp", split_axis=0, concat_axis=1, tiled=True
    ).astype(f32)
    grad_w_up = lax.all_to_all(
        mat_at(mid_all, grad_up_pre).astype(bf16), "dp", split_axis=0, concat_axis=1, tiled=True
    ).astype(f32)

    grad_norm, grad_gain_two = norm_backward(grad_mid, normed_two, rstd_two, gain_two_all)
    grad_hidden = cotangent.astype(f32) + grad_norm
    grad_hidden_b = grad_hidden.astype(bf16)
    grad_mixed = mat_bt(grad_hidden_b, w_out).reshape(count, ways, -1)
    grad_mamba = grad_mixed[:, :, :rows].reshape(count, -1)
    grad_attn = grad_mixed[:, :, rows:].reshape(count, -1)
    grad_w_out = scatter(
        torus, mat_at(mixed, grad_hidden_b).astype(bf16).reshape(all_out.shape), "fold_w_out", 48
    ).astype(f32)
    grad_q, grad_kv = attn_pull(grad_attn)
    grad_z, grad_x, grad_bc, grad_dt, grad_conv, grad_bias, grad_head = mamba_pull(grad_mamba)
    pieces = jnp.concatenate(
        [part.astype(bf16) for part in (grad_z, grad_x, grad_bc, grad_q, grad_kv, grad_dt)]
        + [jnp.zeros((count, extra), bf16)],
        axis=1,
    )
    grad_w_in = scatter(
        torus, mat_at(normed_in, pieces).astype(bf16).reshape(all_in.shape), "fold_w_in", 64
    ).astype(f32)
    grad_normed = mat_bt(pieces, w_in)
    grad_w_z, grad_w_x, grad_w_bc, grad_w_q, grad_w_kv, grad_w_dt = (
        grad_w_in[:, edges[k] : edges[k + 1]] for k in range(6)
    )
    grad_norm, grad_gain_one = norm_backward(grad_normed, normed_one, rstd_one, gain_one_all)
    grad_input = (grad_hidden + grad_norm).astype(bf16)

    totals = lax.psum(
        pack_small((grad_gain_one, grad_gain_two, grad_bias, grad_conv.T, grad_head)), "dp"
    )
    own = lax.axis_index("dp")
    cut = 0
    small_grads = []
    for part in smalls:
        piece = totals[cut : cut + ways * part.size].reshape(ways, part.size)
        piece = lax.dynamic_index_in_dim(piece, own, 0, keepdims=False)
        small_grads.append(piece.reshape(part.shape))
        cut += ways * part.size
    head_total = totals[cut:].reshape(head_params.shape)
    return (
        block_out,
        grad_input,
        small_grads[0],
        grad_w_z,
        grad_w_x,
        grad_w_bc,
        grad_w_dt,
        small_grads[3].T,
        small_grads[2],
        head_total,
        grad_w_out[:rows],
        grad_w_q,
        grad_w_kv,
        grad_w_out[rows:],
        small_grads[1],
        grad_w_gate,
        grad_w_up,
        grad_w_down,
    )


def solution(mesh):
    in_specs = (
        P("dp", None),
        P("dp"),
        P("dp", None),
        P("dp"),
        P("dp", None),
        P("dp", None),
        P("dp", None),
        P("dp", None),
        P(None, "dp"),
        P("dp"),
        P(),
        P("dp", None),
        P("dp", None),
        P("dp", None),
        P("dp", None),
        P("dp"),
        P("dp", None),
        P("dp", None),
        P("dp", None),
    )
    out_specs = (
        P("dp", None),
        P("dp", None),
        P("dp"),
        P("dp", None),
        P("dp", None),
        P("dp", None),
        P("dp", None),
        P(None, "dp"),
        P("dp"),
        P(),
        P("dp", None),
        P("dp", None),
        P("dp", None),
        P("dp", None),
        P("dp"),
        P("dp", None),
        P("dp", None),
        P("dp", None),
    )
    return jax.shard_map(
        functools.partial(per_device, Torus(mesh)), mesh=mesh, in_specs=in_specs, out_specs=out_specs, check_vma=False
    )
```

time: 7840 us -> 2540 us (0.32)
  waiting for transfers between devices: 6940 us -> 17.8 us
  Pallas kernels: 0 us -> 1750 us
  blocking collectives: 160 us -> 0 us
  matrix products: 613 us -> 507 us
  local copies, waits for them, and re-layouts: 49.1 us -> 136 us
    reduce_scatter x10 -> x0, waiting for transfers between devices: 5380 us -> none  [the longest x1 1270 us: per_device(): lax.psum_scatter(ffn_grads[3], 'dp', scatter_dimension=0, tiled=True)]
    pallas_call x0 -> x7, Pallas kernels: none -> 1750 us  [the longest x3 883 us: gather(): pl.pallas_call(functools.partial(gather_kernel, torus, count), out_shape=...]
    all_gather x10 -> x0, waiting for transfers between devices: 1550 us -> none  [the longest x1 384 us: per_device(): lax.all_gather(w_gate, 'dp', axis=0, tiled=True)]
    dot_general x10 -> x5, matrix products: 234 us -> 136 us  [mat_at(): lax.dot_general(left, right, (((0,), (0,)), ((), ())), preferred_element_...]
    unnamed x2 -> x0, blocking collectives: 81.7 us -> none
    dot_general x11 -> x5, matrix products: 161 us -> 176 us  [mat_bt(): lax.dot_general(left, right, (((1,), (1,)), ((), ())), preferred_element_...]
    dot_general x11 -> x5, matrix products: 159 us -> 145 us  [matmul(): return jnp.dot(left, right, preferred_element_type=jnp.float32)]
  transfers between devices with their start and end apart: 22 -> 5, of which waited for: 17 -> 1; matrix products, arithmetic and copies ran while one was open for 7% -> 13% of each run, Pallas kernels for 0% -> 51%
where the time goes in v1:
time: 2540 us; the launch traced here: 2520 us
  Pallas kernels  1750 us (69%)
  matrix products  507 us (20%)
  local copies, waits for them, and re-layouts  136 us (5%)
  other arithmetic  77.2 us (3%)
    pallas_call x3, Pallas kernels, gather(): pl.pallas_call(functools.partial(gather_kernel, torus, count), out_shape=...  883 us
    pallas_call x4, Pallas kernels, scatter(): pl.pallas_call(functools.partial(scatter_kernel, torus, first, size), out...  865 us
    dot_general x5, matrix products, mat_bt(): lax.dot_general(left, right, (((1,), (1,)), ((), ())), preferred_element_...  176 us
    dot_general x5, matrix products, matmul(): return jnp.dot(left, right, preferred_element_type=jnp.float32)  145 us
    dot_general x5, matrix products, mat_at(): lax.dot_general(left, right, (((0,), (0,)), ((), ())), preferred_element_...  136 us
    convert_element_type x1, local copies, waits for them, and re-layouts, per_device(): mat_at(normed_in, pieces).astype(bf16).reshape(all_in.shape)  64.6 us
  transfers between devices with their start and end apart: 5, of which 1 were waited for; matrix products, arithmetic and copies ran while one was open for 13% of the time, Pallas kernels for 51%

profile of v1, /device:TPU:0, one launch (start us, length us, event | category | flops | bytes accessed | tf_op | source)
XLA Modules:
  0.0 2523.7 jit_solution(14693304498262104799)
XLA Ops:
  7.2 3.3 copy.263
  10.6 7.4 all-to-all-start.1
  20.7 1.9 concatenate.46.refs_0_
  22.6 403.0 %spread_weights.1 = (bf16[32,96,8736]{2,1,0:T(8,128)(2,1)}, bf16[32,144,3072]{2,1,0:T(8,128)(2,1)}) custom-call(bf16[96,8736]{1,0:T(8,128)(2,1)} %concatenate.46.refs_0_, bf16[144,3072]{1,0:T(8,128)(2,1)} %pad_maximum_fusion.2.refs_1_), custom_call_target="tpu_custom_call" | custom-call | tf_op jit(solution)/shard_map/spread_weights/pallas_call | solution.py:295
  428.6 29.2 %fusion.74 = f32[256,8736]{0,1:T(8,128)} fusion(bf16[3072,8736]{1,0:T(8,128)(2,1)} %bitcast.331, bf16[256,3072]{1,0:T(8,128)(2,1)S(1)} %copy-done.12, f32[3072]{0:T(1024)S(1)} %reshape.440, f32[256]{0:T(256)S(1)} %add_rsqrt_fusion.1), kind=kOutput, calls=%fused_computation.139 | convolution fusion | flops 13743685632 | bytes 64205824 | tf_op jit(solution)/shard_map/dot_general | solution.py:24
  459.5 4.3 slice.227
  465.5 2.1 slice.225
  467.5 2.0 slice.223
  471.0 3.4 slice_reduce_fusion.3
  474.5 9.9 fusion.23
  491.7 3.0 fusion.60
  494.8 9.9 bitcast_add_fusion.1
  508.1 238.2 %spread_cotangent.1 = bf16[32,256,3072]{2,1,0:T(8,128)(2,1)} custom-call(bf16[256,3072]{1,0:T(8,128)(2,1)} %refs_0_.1), custom_call_target="tpu_custom_call" | custom-call | tf_op jit(solution)/shard_map/spread_cotangent/pallas_call | solution.py:295
  746.4 4.6 convolution_convert_fusion.5
  751.1 3.3 fusion.45
  754.5 13.4 multiply_reduce_fusion.7
  771.1 242.0 %spread_mid.1 = bf16[32,256,3072]{2,1,0:T(8,128)(2,1)} custom-call(bf16[256,3072]{1,0:T(8,128)(2,1)} %multiply_convert_fusion.3.refs_0_), custom_call_target="tpu_custom_call" | custom-call | tf_op jit(solution)/shard_map/spread_mid/pallas_call | solution.py:295
  1014.2 5.8 all-to-all-start
  1022.9 33.7 %fusion.126 = f32[8192,384]{1,0:T(8,128)} fusion(bf16[8192,3072]{1,0:T(8,128)(2,1)} %bitcast.290, bf16[3072,384]{1,0:T(8,128)(2,1)} %bitcast.29), kind=kOutput, calls=%fused_computation.249 | convolution fusion | flops 19327352832 | bytes 65273856 | tf_op jit(solution)/shard_map/dot_general | solution.py:24
  1056.6 17.8 all-to-all-done
  1074.4 34.0 %fusion.125 = f32[8192,384]{1,0:T(8,128)} fusion(bf16[8192,3072]{1,0:T(8,128)(2,1)} %bitcast.291, bf16[3072,384]{1,0:T(8,128)(2,1)} %bitcast.27), kind=kOutput, calls=%fused_computation.248 | convolution fusion | flops 19327352832 | bytes 65273856 | tf_op jit(solution)/shard_map/dot_general | solution.py:24
  1108.4 41.3 %multiply_convert_fusion = (bf16[8192,384]{1,0:T(8,128)(2,1)}, bf16[8192,384]{1,0:T(8,128)(2,1)}, bf16[8192,384]{1,0:T(8,128)(2,1)}) fusion(f32[8192,384]{1,0:T(8,128)} %fusion.125, f32[8192,384]{1,0:T(8,128)} %fusion.126, bf16[8192,3072]{1,0:T(8,128)(2,1)} %bitcast.288, bf16[384,3072]{1,0:T(8,128)(2,1)S(1)} %copy-done.105), kind=kOutput, calls=%fused_computation.4 | convolution fusion | flops 19377684480 | bytes 96731136 | tf_op jit(solution)/shard_map/dot_general | solution.py:28
  1149.7 34.1 %convolution_convert_fusion.4 = bf16[3072,384]{1,0:T(8,128)(2,1)} fusion(bf16[8192,3072]{1,0:T(8,128)(2,1)} %bitcast.292, bf16[8192,384]{1,0:T(8,128)(2,1)} %get-tuple-element.158), kind=kOutput, calls=%fused_computation.31 | convolution fusion | flops 19328532480 | bytes 58982400 | tf_op jit(solution)/shard_map/dot_general | solution.py:34
  1183.7 41.0 %fusion.127 = f32[8192,3072]{1,0:T(8,128)} fusion(bf16[8192,384]{1,0:T(8,128)(2,1)} %get-tuple-element.158, bf16[3072,384]{1,0:T(8,128)(2,1)} %bitcast.27), kind=kOutput, calls=%fused_computation.250 | convolution fusion | flops 19327352832 | bytes 109314048 | tf_op jit(solution)/shard_map/dot_general | solution.py:28
  1224.8 34.6 %convolution_convert_fusion.1 = bf16[8192,3072]{1,0:T(8,128)(2,1)} fusion(bf16[8192,384]{1,0:T(8,128)(2,1)} %get-tuple-element.159, bf16[384,3072]{1,0:T(8,128)(2,1)S(1)} %copy-done.105), kind=kOutput, calls=%fused_computation.2 | convolution fusion | flops 19352518656 | bytes 58982400 | tf_op jit(solution)/shard_map/dot_general | solution.py:24
  1259.4 235.5 %fold_out_0.1 = bf16[256,3072]{1,0:T(8,128)(2,1)} custom-call(bf16[32,256,3072]{2,1,0:T(8,128)(2,1)} %bitcast.294), custom_call_target="tpu_custom_call" | custom-call | tf_op jit(solution)/shard_map/fold_out_0/pallas_call | solution.py:410
  1494.8 54.1 %add_convert_fusion = bf16[8192,3072]{1,0:T(8,128)(2,1)} fusion(f32[8192,3072]{1,0:T(8,128)} %fusion.127, bf16[8192,384]{1,0:T(8,128)(2,1)} %get-tuple-element.157, bf16[3072,384]{1,0:T(8,128)(2,1)} %bitcast.29), kind=kOutput, calls=%fused_computation | convolution fusion | flops 19377684480 | bytes 159645696 | tf_op jit(solution)/shard_map/dot_general | solution.py:28
  1548.9 233.9 %fold_mid_0.1 = bf16[256,3072]{1,0:T(8,128)(2,1)} custom-call(bf16[32,256,3072]{2,1,0:T(8,128)(2,1)} %bitcast.281), custom_call_target="tpu_custom_call" | custom-call | tf_op jit(solution)/shard_map/fold_mid_0/pallas_call | solution.py:410
  1782.8 3.6 fusion.27
  1786.6 5.7 fusion.26
  1792.3 15.5 fusion.66
  1811.7 4.4 multiply_reduce_fusion.4
  1816.2 9.7 fusion.17
  1825.9 7.5 fusion.44
  1835.0 4.6 fusion.70
  1839.6 3.6 multiply_reduce_fusion.6
  1846.0 3.1 convolution_bitcast_fusion.1
  1849.1 2.0 fusion.86
  1851.2 2.5 reduce-window.16
  1856.3 3.5 bitcast_add_fusion
  1861.3 9.1 multiply_reduce_fusion.3
  1870.5 2.1 fusion.20
  1872.7 2.1 fusion.21
  1874.9 2.3 fusion.22
  1879.4 2.7 fusion.65
  1884.9 24.2 fusion.34
  1909.1 24.1 convolution_convert_fusion
  1933.2 4.2 all-to-all-start.2
  1940.5 2.9 reshape.426
  1944.1 14.9 convolution_convert_fusion.2
  1959.0 64.6 %copy.218 = bf16[3072,8736]{1,0:T(8,128)(2,1)} copy(bf16[3072,8736]{0,1:T(8,128)(2,1)} %convolution_convert_fusion) | data formatting | bytes 107347968 | tf_op jit(solution)/shard_map/convert_element_type | solution.py:565
  2023.6 253.4 %fold_w_in_0.1 = bf16[96,8736]{1,0:T(8,128)(2,1)} custom-call(bf16[32,96,8736]{2,1,0:T(8,128)(2,1)} %bitcast.280), custom_call_target="tpu_custom_call" | custom-call | tf_op jit(solution)/shard_map/fold_w_in_0/pallas_call | solution.py:410
  2277.0 5.5 fusion.33
  2282.6 34.1 %convolution_convert_fusion.3 = bf16[3072,384]{1,0:T(8,128)(2,1)} fusion(bf16[8192,3072]{1,0:T(8,128)(2,1)} %bitcast.293, bf16[8192,384]{1,0:T(8,128)(2,1)} %get-tuple-element.157), kind=kOutput, calls=%fused_computation.30 | convolution fusion | flops 19328532480 | bytes 58982400 | tf_op jit(solution)/shard_map/dot_general | solution.py:34
  2316.7 3.8 all-to-all-start.3
  2322.2 28.7 %fusion.128 = f32[384,3072]{1,0:T(8,128)} fusion(bf16[8192,384]{1,0:T(8,128)(2,1)} %get-tuple-element.159, bf16[8192,3072]{1,0:T(8,128)(2,1)} %bitcast.289), kind=kOutput, calls=%fused_computation.251 | convolution fusion | flops 19327352832 | bytes 61341696 | tf_op jit(solution)/shard_map/dot_general | solution.py:34
  2351.7 142.3 %fold_w_out_0.1 = bf16[144,3072]{1,0:T(8,128)(2,1)} custom-call(bf16[32,144,3072]{2,1,0:T(8,128)(2,1)} %bitcast.282), custom_call_target="tpu_custom_call" | custom-call | tf_op jit(solution)/shard_map/fold_w_out_0/pallas_call | solution.py:410
  2493.9 1.8 slice.259
  2495.8 2.2 slice.256
  2498.7 1.8 slice.257
  2506.9 2.2 convert_bitcast_fusion.1
  2509.2 2.6 copy.253
  2511.8 2.2 convert_bitcast_fusion
  2514.0 2.6 copy.254
  (354 shorter events, 58.8 us)
Async XLA Ops:
  10.5 7.6 copy-start.77
  10.5 8.6 copy-start.86
  10.5 8.7 copy-start.98
  10.5 8.9 copy-start.99
  10.5 8.9 copy-start.100
  10.5 8.9 copy-start.101
  10.6 9.1 copy-start.45
  10.6 9.1 copy-start.50
  10.6 10.1 copy-start.46
  10.6 10.1 copy-start.47
  10.6 10.1 copy-start.51
  10.6 10.1 copy-start.75
  10.6 10.1 copy-start.76
  10.6 1003.6 %all-to-all-start.1 = ((bf16[96,32,384]{2,0,1:T(8,128)(2,1)}), bf16[96,32,384]{2,0,1:T(8,128)(2,1)}, u32[]{:S(2)}, u32[]{:S(2)}) async-start(bf16[96,32,384]{2,0,1:T(8,128)(2,1)} %bitcast.277), calls=%async_computation.1 | async-start | bytes 4718592 | tf_op jit(solution)/shard_map/all_to_all | solution.py:524
  19.1 475.7 %copy-start.58 = (pred[256,256]{1,0:T(8,128)(4,1)}, pred[256,256]{1,0:T(8,128)(4,1)S(1)}, u32[]{:S(2)}) copy-start(pred[256,256]{1,0:T(8,128)(4,1)S(1)} %get-tuple-element.194) | copy-start | bytes 196612
  428.4 29.3 %copy-start.84 = (f32[256]{0:T(256)}, f32[256]{0:T(256)S(1)}, u32[]{:S(2)}) copy-start(f32[256]{0:T(256)S(1)} %add_rsqrt_fusion.1) | copy-start | bytes 3076
  428.6 29.2 %copy-start.71 = (f32[3072]{0:T(1024)}, f32[3072]{0:T(1024)S(1)}, u32[]{:S(2)}) copy-start(f32[3072]{0:T(1024)S(1)} %reshape.440) | copy-start | bytes 36868
  459.5 6.0 copy-start
  469.7 4.9 copy-start.91
  474.4 10.1 copy-start.62
  474.4 10.1 copy-start.64
  474.4 10.1 copy-start.66
  474.4 10.1 copy-start.68
  474.5 31.0 %copy-start.95 = (pred[256]{0:T(512)(128)(4,1)}, pred[256]{0:T(512)(128)(4,1)S(1)}, u32[]{:S(2)}) copy-start(pred[256]{0:T(512)(128)(4,1)S(1)} %pad_add_fusion.2) | copy-start | bytes 772
  486.5 8.3 copy-start.55
  489.1 257.3 %copy-start.33 = (pred[256,256]{0,1:T(8,128)(4,1)}, pred[256,256]{0,1:T(8,128)(4,1)S(1)}, u32[]{:S(2)}) copy-start(pred[256,256]{0,1:T(8,128)(4,1)S(1)} %copy.197) | copy-start | bytes 196612
  490.0 4.8 copy-start.73
  494.8 10.0 copy-start.1
  494.8 251.7 %copy-start.48 = (f32[2,6,256]{2,1,0:T(8,128)}, f32[2,6,256]{2,1,0:T(8,128)S(1)}, u32[]{:S(2)}) copy-start(f32[2,6,256]{2,1,0:T(8,128)S(1)} %get-tuple-element.195) | copy-start | bytes 36868
  505.5 516.8 %copy-start.52 = (f32[2,6,256]{2,1,0:T(8,128)}, f32[2,6,256]{2,1,0:T(8,128)S(1)}, u32[]{:S(2)}) copy-start(f32[2,6,256]{2,1,0:T(8,128)S(1)} %fusion.103) | copy-start | bytes 36868
  746.4 21.5 copy-start.60
  754.4 13.4 copy-start.16
  767.9 245.2 %copy-start.82 = (f32[256]{0:T(256)}, f32[256]{0:T(256)S(1)}, u32[]{:S(2)}) copy-start(f32[256]{0:T(256)S(1)} %add_rsqrt_fusion) | copy-start | bytes 3076
  1013.1 6.9 copy-start.17
  1014.2 60.2 %all-to-all-start = ((bf16[96,32,384]{2,0,1:T(8,128)(2,1)}), bf16[96,32,384]{2,0,1:T(8,128)(2,1)}, u32[]{:S(2)}, u32[]{:S(2)}) async-start(bf16[96,32,384]{2,0,1:T(8,128)(2,1)} %bitcast.303), calls=%async_computation | async-start | bytes 4718592 | tf_op jit(solution)/shard_map/all_to_all | solution.py:523
  1074.4 34.0 %copy-start.105 = (bf16[384,3072]{1,0:T(8,128)(2,1)S(1)}, bf16[384,3072]{1,0:T(8,128)(2,1)}, u32[]{:S(2)}) copy-start(bf16[384,3072]{1,0:T(8,128)(2,1)} %param.37) | copy-start | bytes 7077892
  1548.9 233.9 %copy-start.61 = (f32[3072]{0:T(1024)S(1)}, f32[3072]{0:T(1024)}, u32[]{:S(2)}) copy-start(f32[3072]{0:T(1024)} %copy-done.60) | copy-start | bytes 36868
  1548.9 233.9 %copy-start.83 = (f32[256]{0:T(256)S(1)}, f32[256]{0:T(256)}, u32[]{:S(2)}) copy-start(f32[256]{0:T(256)} %copy-done.82) | copy-start | bytes 3076
  1786.6 22.9 slice-start
  1792.3 17.2 slice-start.1
  1792.3 17.3 slice-start.2
  1816.1 9.7 copy-start.21
  1825.9 9.1 copy-start.2
  1825.9 9.1 copy-start.34
  1825.9 9.1 copy-start.49
  1825.9 9.1 copy-start.53
  1849.1 6.1 copy-start.36
  1849.1 6.0 copy-start.38
  1851.1 5.2 copy-start.79
  1856.3 5.0 copy-start.8
  1856.3 5.0 copy-start.92
  1856.3 5.0 copy-start.94
  1856.3 5.0 copy-start.96
  1861.3 9.1 copy-start.69
  1861.3 9.1 copy-start.102
  1872.7 5.9 slice-start.3
  1872.7 5.9 slice-start.4
  1879.3 5.6 copy-start.14
  1879.3 5.6 copy-start.72
  1879.4 5.6 copy-start.85
  1933.2 383.4 %all-to-all-start.2 = ((bf16[32,96,384]{2,1,0:T(8,128)(2,1)}), bf16[32,96,384]{2,1,0:T(8,128)(2,1)}, u32[]{:S(2)}, u32[]{:S(2)}) async-start(bf16[32,96,384]{2,1,0:T(8,128)(2,1)} %bitcast.317), calls=%async_computation.2 | async-start | bytes 4718592 | tf_op jit(solution)/shard_map/all_to_all | solution.py:541
  1937.4 6.7 copy-start.11
  1937.5 563.7 %all-reduce.27.cloned.1.call-start = ((), (), s32[]{:S(2)}) async-start(), calls=%async_computation.4 | async-start | bytes 196608 | tf_op jit(solution)/shard_map/psum | solution.py:574
  2316.7 195.1 %all-to-all-start.3 = ((bf16[32,96,384]{2,1,0:T(8,128)(2,1)}), bf16[32,96,384]{2,1,0:T(8,128)(2,1)}, u32[]{:S(2)}, u32[]{:S(2)}) async-start(bf16[32,96,384]{2,1,0:T(8,128)(2,1)} %bitcast.318), calls=%async_computation.3 | async-start | bytes 4718592 | tf_op jit(solution)/shard_map/all_to_all | solution.py:544
  (55 other events, 170.0 us)
Sparse Core Ops, SparseCore 0:
  1944.4 132.0 all-reduce.26

commit v2 on v1

--- a/solution.py
+++ b/solution.py
@@ -4,8 +4,10 @@
 import jax.numpy as jnp
 from jax import lax
 from jax.experimental import pallas as pl
+from jax.experimental.layout import Layout, with_layout_constraint
 from jax.experimental.pallas import tpu as pltpu
 from jax.sharding import PartitionSpec as P
+
 
 HEADS = 24
 HDIM = 128
@@ -116,7 +118,7 @@
     return scanned.reshape(count, DSSM) * jax.nn.silu(z_part)
 
 
-VMEM_LIMIT = 66000000
+VMEM_LIMIT = 67000000
 
 
 class Torus:
@@ -236,21 +238,28 @@
     ]
     for copy in own_copies:
         copy.start()
-    for k, i, j in torus.order():
-        block = place.at(k, i, j)
-        own = (k, i, j) == (0, 0, 0)
-        if not own:
-            arrive(block)
-        if own:
-            for step in range(1, torus.nz):
-                push(block, place.at(step, 0, 0), own)
-        if i == 0 and j == 0:
-            for step in range(1, torus.n2):
-                push(block, place.at(0, step, 0), own)
-        if j == 0:
+    late = []
+    for k in range(torus.nz):
+        for i in range(torus.n2):
+            block, own = place.at(k, i, 0), (k, i) == (0, 0)
+            if own:
+                for step in range(1, torus.nz):
+                    push(block, place.at(step, 0, 0), own)
+            else:
+                arrive(block)
+            if i == 0:
+                for step in range(1, torus.n2):
+                    push(block, place.at(0, step, 0), own)
             for step in range(1, torus.n3):
                 push(block, place.at(0, 0, step), own)
-        push(block, place.sibling, own)
+            push(block, place.sibling, own)
+            for block in late:
+                arrive(block)
+                push(block, place.sibling)
+            late = [place.at(k, i, j) for j in range(1, torus.n3)]
+    for block in late:
+        arrive(block)
+        push(block, place.sibling)
     for copy in own_copies:
         copy.wait()
     for k, i, j in torus.order():
@@ -290,7 +299,7 @@
     spread(torus, place, ins, outs, send_sem, recv_sem, local_sem)
 
 
-def gather(torus, arrays, name, ident):
+def gather(torus, arrays, ident):
     count, n = len(arrays), torus.n
     return pl.pallas_call(
         functools.partial(gather_kernel, torus, count),
@@ -305,12 +314,42 @@
         compiler_params=pltpu.CompilerParams(
             collective_id=ident, has_side_effects=True, vmem_limit_bytes=VMEM_LIMIT
         ),
-        name=name,
     )(*arrays)
 
 
-def scatter_kernel(torus, first, wide, part_ref, out_ref, stage, from_core, from_third, from_second,
-                   from_z, load_sem, core_sem, third_sem, second_sem, z_sem, send_sem):
+def add(into, term):
+    rows = into.shape[0]
+    step = 16
+    if rows % step:
+        into[...] = (into[...].astype(jnp.float32) + term[...].astype(jnp.float32)).astype(into.dtype)
+        return
+
+    @pl.loop(0, rows // step)
+    def _(index):
+        piece = pl.ds(pl.multiple_of(index * step, step), step)
+        into[piece, :] = (
+            into[piece, :].astype(jnp.float32) + term[piece, :].astype(jnp.float32)
+        ).astype(into.dtype)
+
+
+def scatter_kernel(
+    torus,
+    first,
+    wide,
+    part_ref,
+    out_ref,
+    stage,
+    from_core,
+    from_third,
+    from_second,
+    from_z,
+    load_sem,
+    core_sem,
+    third_sem,
+    second_sem,
+    z_sem,
+    send_sem,
+):
     place = Place(torus)
     greet(place)
     nz, n2, n3 = torus.nz, torus.n2, torus.n3
@@ -367,38 +406,23 @@
             add(from_core.at[s], from_second.at[t])
         if k:
             send(from_core.at[s], from_z.at[k - 1], z_sem.at[k - 1], place.at(k, 0, 0))
+    out_ref[...] = from_core[0].astype(out_ref.dtype)
     for k in range(1, nz):
         receive(from_z.at[k - 1], z_sem.at[k - 1])
-        add(from_core.at[0], from_z.at[k - 1])
-    out_ref[...] = from_core[0]
+        add(out_ref, from_z.at[k - 1])
     for copy in started:
         copy.wait_send()
 
 
-def add(into, term):
-    rows = into.shape[0]
-    step = 16
-    if rows % step:
-        into[...] = (into[...].astype(jnp.float32) + term[...].astype(jnp.float32)).astype(into.dtype)
-        return
-
-    @pl.loop(0, rows // step)
-    def _(index):
-        piece = pl.ds(pl.multiple_of(index * step, step), step)
-        into[piece, :] = (
-            into[piece, :].astype(jnp.float32) + term[piece, :].astype(jnp.float32)
-        ).astype(into.dtype)
-
-
-def scatter(torus, part, name, ident):
-    n, rows, width = part.shape
+def scatter(torus, part, ident):
+    _, rows, width = part.shape
     nz, n2, n3 = torus.nz, torus.n2, torus.n3
     thirds, seconds = nz * n2 * (n3 - 1), nz * (n2 - 1)
-    blocks = nz * n2 * n3 + thirds + seconds + nz - 1 + 3
+    blocks = nz * n2 * n3 + thirds + seconds + nz - 1 + 4
     lanes = -(-width // 128)
     tile = (-(-rows // 16) * 16) * 128 * part.dtype.itemsize
     pieces = 1
-    while blocks * tile * -(-lanes // pieces) > VMEM_LIMIT - 6 * 2**20:
+    while blocks * tile * -(-lanes // pieces) > VMEM_LIMIT - 2**20:
         pieces += 1
     wide = -(-lanes // pieces) * 128
     outs = []
@@ -409,7 +433,7 @@
         outs.append(
             pl.pallas_call(
                 functools.partial(scatter_kernel, torus, first, size),
-                out_shape=jax.ShapeDtypeStruct(block, part.dtype),
+                out_shape=jax.ShapeDtypeStruct(block, jnp.float32),
                 in_specs=[pl.BlockSpec(memory_space=pl.ANY)],
                 out_specs=pl.BlockSpec(memory_space=pltpu.VMEM),
                 scratch_shapes=[
@@ -428,10 +452,60 @@
                 compiler_params=pltpu.CompilerParams(
                     collective_id=ident + number, has_side_effects=True, vmem_limit_bytes=VMEM_LIMIT
                 ),
-                name=f"{name}_{number}",
             )(part)
         )
     return outs[0] if len(outs) == 1 else jnp.concatenate(outs, axis=1)
+
+
+def ffn_kernel(units, mid_ref, cot_ref, pair_ref, down_ref, act_ref, grad_ref, mid_share_ref, out_share_ref):
+    f32, bf16 = jnp.float32, jnp.bfloat16
+    pre = jnp.dot(mid_ref[...], pair_ref[...], preferred_element_type=f32)
+    grad_act = mat_bt(cot_ref[...], down_ref[...])
+    gate, up = pre[:, :units], pre[:, units : 2 * units]
+    sigma = jax.nn.sigmoid(gate)
+    act = (gate * sigma * up).astype(bf16)
+    act_ref[...] = act
+    grad_ref[:, :units] = (grad_act * up * sigma * (1.0 + gate * (1.0 - sigma))).astype(bf16)
+    grad_ref[:, units:] = (grad_act * gate * sigma).astype(bf16)
+    mid_share_ref[...] = mat_bt(grad_ref[...], pair_ref[...]).astype(bf16)
+    out_share_ref[...] = jnp.dot(act, down_ref[...], preferred_element_type=f32).astype(bf16)
+
+
+def feed_forward(mid, cot, pair, down, step):
+    tokens, width = mid.shape
+    units = down.shape[0]
+    bf16 = jnp.bfloat16
+    whole = lambda i: (0, 0)
+    part = lambda i: (i, 0)
+    return pl.pallas_call(
+        functools.partial(ffn_kernel, units),
+        grid=(tokens // step,),
+        out_shape=[
+            jax.ShapeDtypeStruct((tokens, units), bf16),
+            jax.ShapeDtypeStruct((tokens, 2 * units), bf16),
+            jax.ShapeDtypeStruct((tokens, width), bf16),
+            jax.ShapeDtypeStruct((tokens, width), bf16),
+        ],
+        in_specs=[
+            pl.BlockSpec((step, width), part),
+            pl.BlockSpec((step, width), part),
+            pl.BlockSpec(pair.shape, whole, pipeline_mode=pl.Buffered(1)),
+            pl.BlockSpec(down.shape, whole, pipeline_mode=pl.Buffered(1)),
+        ],
+        out_specs=[
+            pl.BlockSpec((step, units), part),
+            pl.BlockSpec((step, 2 * units), part),
+            pl.BlockSpec((step, width), part),
+            pl.BlockSpec((step, width), part),
+        ],
+        compiler_params=pltpu.CompilerParams(vmem_limit_bytes=VMEM_LIMIT),
+        cost_estimate=pl.CostEstimate(
+            flops=12 * tokens * width * units,
+            bytes_accessed=8 * tokens * width,
+            transcendentals=tokens * units,
+        ),
+        name="feed_forward",
+    )(mid, cot, pair, down)
 
 
 def pack_small(parts):
@@ -483,7 +557,7 @@
         edges.append(edges[-1] + w.shape[1])
     share_in = jnp.concatenate(projections + (packed,), axis=1)
     share_out = jnp.concatenate([w_mout, w_ao], axis=0)
-    all_in, all_out = gather(torus, [share_in, share_out], "spread_weights", 1)
+    all_in, all_out = gather(torus, [share_in, share_out], 1)
     packed_all = all_in[:, :, edges[-1] :].reshape(ways, -1)
     w_in = all_in.reshape(ways * rows, -1)
     w_out = all_out.reshape(-1, width)
@@ -520,40 +594,34 @@
     hidden = as_float + matmul(mixed, w_out)
     normed_two, rstd_two, normed_mid = norm_forward(hidden, gain_two_all)
 
-    w_gate_own = lax.all_to_all(w_gate, "dp", split_axis=1, concat_axis=0, tiled=True)
-    w_up_own = lax.all_to_all(w_up, "dp", split_axis=1, concat_axis=0, tiled=True)
-    cot_all = gather(torus, [cotangent], "spread_cotangent", 2)[0].reshape(-1, width)
-    mid_all = gather(torus, [normed_mid], "spread_mid", 3)[0].reshape(-1, width)
-    gate_pre = matmul(mid_all, w_gate_own)
-    up_pre = matmul(mid_all, w_up_own)
-    sigma = jax.nn.sigmoid(gate_pre)
-    activated = (gate_pre * sigma * up_pre).astype(bf16)
-    grad_act = mat_bt(cot_all, w_down)
-    grad_up_pre = (grad_act * gate_pre * sigma).astype(bf16)
-    grad_gate_pre = (grad_act * up_pre * sigma * (1.0 + gate_pre * (1.0 - sigma))).astype(bf16)
-    mid_share = (mat_bt(grad_gate_pre, w_gate_own) + mat_bt(grad_up_pre, w_up_own)).astype(bf16)
-    out_share = matmul(activated, w_down).astype(bf16)
-    blocks = (ways, count, width)
-    grad_mid = scatter(torus, mid_share.reshape(blocks), "fold_mid", 16).astype(f32)
-    out_sum = scatter(torus, out_share.reshape(blocks), "fold_out", 32)
-    block_out = (hidden + out_sum.astype(f32)).astype(bf16)
+    hidden_units = w_gate.shape[1] // ways
+    w_pair = jnp.concatenate(
+        [w.reshape(rows, ways, hidden_units) for w in (w_gate, w_up)], axis=2
+    ).reshape(rows, -1)
+    w_pair = lax.all_to_all(w_pair, "dp", split_axis=1, concat_axis=0, tiled=True)
+    cot_own, packed_all = lax.optimization_barrier((cotangent, packed_all))
+    cot_all = lax.all_gather(cot_own, "dp", axis=0, tiled=True)
+    mid_all = gather(torus, [normed_mid], 3)[0].reshape(-1, width)
+    activated, grad_pre, mid_share, out_share = feed_forward(mid_all, cot_all, w_pair, w_down, 2 * count)
+    out_sum = lax.psum_scatter(out_share, "dp", scatter_dimension=0, tiled=True)
+    grad_mid = scatter(torus, mid_share.reshape(ways, count, width), 16)
     grad_w_down = mat_at(activated, cot_all)
-    grad_w_gate = lax.all_to_all(
-        mat_at(mid_all, grad_gate_pre).astype(bf16), "dp", split_axis=0, concat_axis=1, tiled=True
-    ).astype(f32)
-    grad_w_up = lax.all_to_all(
-        mat_at(mid_all, grad_up_pre).astype(bf16), "dp", split_axis=0, concat_axis=1, tiled=True
-    ).astype(f32)
+    grad_pair = mat_at(mid_all, grad_pre).astype(bf16)
+    grad_mid, grad_pair, grad_w_down = lax.optimization_barrier((grad_mid, grad_pair, grad_w_down))
+    grad_pair = lax.all_to_all(grad_pair, "dp", split_axis=0, concat_axis=1, tiled=True)
+    grad_pair = grad_pair.reshape(rows, ways, 2, hidden_units)
+    grad_w_gate = grad_pair[:, :, 0].reshape(rows, -1).astype(f32)
+    grad_w_up = grad_pair[:, :, 1].reshape(rows, -1).astype(f32)
 
     grad_norm, grad_gain_two = norm_backward(grad_mid, normed_two, rstd_two, gain_two_all)
     grad_hidden = cotangent.astype(f32) + grad_norm
     grad_hidden_b = grad_hidden.astype(bf16)
-    grad_mixed = mat_bt(grad_hidden_b, w_out).reshape(count, ways, -1)
+    grad_mixed = mat_bt(grad_hidden_b, w_out)
+    grad_mixed = grad_mixed.reshape(count, ways, -1)
     grad_mamba = grad_mixed[:, :, :rows].reshape(count, -1)
     grad_attn = grad_mixed[:, :, rows:].reshape(count, -1)
-    grad_w_out = scatter(
-        torus, mat_at(mixed, grad_hidden_b).astype(bf16).reshape(all_out.shape), "fold_w_out", 48
-    ).astype(f32)
+    grad_w_out = mat_at(mixed, grad_hidden_b).astype(bf16).reshape(all_out.shape)
+    grad_w_out = scatter(torus, grad_w_out, 48)
     grad_q, grad_kv = attn_pull(grad_attn)
     grad_z, grad_x, grad_bc, grad_dt, grad_conv, grad_bias, grad_head = mamba_pull(grad_mamba)
     pieces = jnp.concatenate(
@@ -561,15 +629,18 @@
         + [jnp.zeros((count, extra), bf16)],
         axis=1,
     )
-    grad_w_in = scatter(
-        torus, mat_at(normed_in, pieces).astype(bf16).reshape(all_in.shape), "fold_w_in", 64
-    ).astype(f32)
+    pieces = with_layout_constraint(pieces, Layout((1, 0)))
+    upright = with_layout_constraint(lax.optimization_barrier(pieces), Layout((0, 1)))
+    grad_w_in = with_layout_constraint(mat_at(normed_in, upright).astype(bf16), Layout((0, 1)))
+    grad_w_in = scatter(torus, grad_w_in.reshape(all_in.shape), 64)
     grad_normed = mat_bt(pieces, w_in)
     grad_w_z, grad_w_x, grad_w_bc, grad_w_q, grad_w_kv, grad_w_dt = (
         grad_w_in[:, edges[k] : edges[k + 1]] for k in range(6)
     )
     grad_norm, grad_gain_one = norm_backward(grad_normed, normed_one, rstd_one, gain_one_all)
     grad_input = (grad_hidden + grad_norm).astype(bf16)
+    late, grad_input = lax.optimization_barrier((hidden, grad_input))
+    block_out = (late + out_sum.astype(f32)).astype(bf16)
 
     totals = lax.psum(
         pack_small((grad_gain_one, grad_gain_two, grad_bias, grad_conv.T, grad_head)), "dp"

time: 2540 us -> 2270 us (0.89)
  matrix products: 507 us -> 250 us
  waiting for transfers between devices: 17.8 us -> 113 us
  Pallas kernels: 1750 us -> 1680 us
  local copies, waits for them, and re-layouts: 136 us -> 110 us
    pallas_call x0 -> x1, Pallas kernels: none -> 166 us  [feed_forward(): pl.pallas_call(functools.partial(ffn_kernel, units), grid=(tokens // step...]
    dot_general x5 -> x2, matrix products: 176 us -> 39.8 us  [mat_bt(): lax.dot_general(left, right, (((1,), (1,)), ((), ())), preferred_element_...]
    pallas_call x3 -> x2, Pallas kernels: 883 us -> 758 us  [gather(): pl.pallas_call(functools.partial(gather_kernel, torus, count), out_shape=...]
    reduce_scatter x0 -> x1, waiting for transfers between devices: none -> 113 us  [per_device(): out_sum = lax.psum_scatter(out_share, 'dp', scatter_dimension=0, tiled=True)]
    pallas_call x4 -> x3, Pallas kernels: 865 us -> 760 us  [scatter(): pl.pallas_call(functools.partial(scatter_kernel, torus, first, size), out...]
    dot_general x5 -> x2, matrix products: 145 us -> 43.5 us  [matmul(): return jnp.dot(left, right, preferred_element_type=jnp.float32)]
    convert_element_type x3 -> x0, local copies, waits for them, and re-layouts: 69.8 us -> none  [the longest x1 64.6 us: per_device(): mat_at(normed_in, pieces).astype(bf16).reshape(all_in.shape)]
    dot_general x5 -> x4, matrix products: 136 us -> 120 us  [mat_at(): lax.dot_general(left, right, (((0,), (0,)), ((), ())), preferred_element_...]
  transfers between devices with their start and end apart: 5 -> 5, of which waited for: 1 -> 1; matrix products, arithmetic and copies ran while one was open for 13% -> 10% of each run, Pallas kernels for 51% -> 40%
where the time goes in v2:
time: 2270 us; the launch traced here: 2260 us
  Pallas kernels  1680 us (74%)
  matrix products  250 us (11%)
  waiting for transfers between devices  113 us (5%)
  local copies, waits for them, and re-layouts  110 us (5%)
  other arithmetic  79.8 us (4%)
    pallas_call x3, Pallas kernels, scatter(): pl.pallas_call(functools.partial(scatter_kernel, torus, first, size), out...  760 us
    pallas_call x2, Pallas kernels, gather(): pl.pallas_call(functools.partial(gather_kernel, torus, count), out_shape=...  758 us
    pallas_call x1, Pallas kernels, feed_forward(): pl.pallas_call(functools.partial(ffn_kernel, units), grid=(tokens // step...  166 us
    dot_general x4, matrix products, mat_at(): lax.dot_general(left, right, (((0,), (0,)), ((), ())), preferred_element_...  120 us
    reduce_scatter x1, waiting for transfers between devices, per_device(): out_sum = lax.psum_scatter(out_share, 'dp', scatter_dimension=0, tiled=True)  113 us
  transfers between devices with their start and end apart: 5, of which 1 were waited for; matrix products, arithmetic and copies ran while one was open for 10% of the time, Pallas kernels for 40%

profile of v2, /device:TPU:0, one launch (start us, length us, event | category | flops | bytes accessed | tf_op | source)
XLA Modules:
  0.0 2261.8 jit_solution(6989030275964823582)
XLA Ops:
  9.8 2.1 pad_maximum_fusion.3.refs_1_
  12.0 3.7 concatenate.49.refs_0_
  15.7 377.8 %shard_map.322 = (bf16[32,96,8736]{2,1,0:T(8,128)(2,1)}, bf16[32,144,3072]{2,1,0:T(8,128)(2,1)}) custom-call(bf16[96,8736]{1,0:T(8,128)(2,1)} %concatenate.49.refs_0_, bf16[144,3072]{1,0:T(8,128)(2,1)} %pad_maximum_fusion.3.refs_1_), custom_call_target="tpu_custom_call" | custom-call | tf_op jit(solution)/shard_map/pallas_call | solution.py:304
  396.6 2.2 copy_bitcast_fusion
  398.7 2.8 pad_maximum_fusion
  401.6 3.9 all-to-all-start
  406.9 29.3 %fusion.68 = f32[256,8736]{0,1:T(8,128)} fusion(bf16[3072,8736]{1,0:T(8,128)(2,1)} %bitcast.311, bf16[256,3072]{1,0:T(8,128)(2,1)S(1)} %copy-done.13, f32[3072]{0:T(1024)S(1)} %reshape.441, f32[256]{0:T(256)S(1)} %add_rsqrt_fusion.1), kind=kOutput, calls=%fused_computation.128 | convolution fusion | flops 13743685632 | bytes 64205824 | tf_op jit(solution)/shard_map/dot_general | solution.py:26
  436.2 4.3 slice.231
  440.5 4.8 slice.233
  445.3 2.0 slice.235
  449.9 3.4 slice_reduce_fusion.3
  453.4 10.9 fusion.21
  465.0 2.2 slice.236
  470.0 1.8 fusion.113
  472.4 1.7 copy.214
  480.0 2.0 fusion.75
  482.2 3.0 fusion.54
  486.0 8.0 bitcast_add_fusion.1
  494.0 2.5 convolution_convert_fusion.3
  497.5 14.2 multiply_reduce_fusion.9
  511.8 1.6 copy-done.1
  515.0 380.6 %shard_map.323 = bf16[32,256,3072]{2,1,0:T(8,128)(2,1)} custom-call(bf16[256,3072]{1,0:T(8,128)(2,1)} %multiply_convert_fusion.refs_0_), custom_call_target="tpu_custom_call" | custom-call | tf_op jit(solution)/shard_map/pallas_call | solution.py:304
  898.0 165.7 %feed_forward.1 = (bf16[8192,384]{1,0:T(8,128)(2,1)}, bf16[8192,768]{1,0:T(8,128)(2,1)}, bf16[8192,3072]{1,0:T(8,128)(2,1)}, bf16[8192,3072]{1,0:T(8,128)(2,1)}) custom-call(bf16[8192,3072]{1,0:T(8,128)(2,1)} %bitcast.272, bf16[8192,3072]{1,0:T(8,128)(2,1)} %all-gather.2.cloned.1.call-done.cot_ref, bf16[3072,768]{1,0:T(8,128)(2,1)} %bitcast.27.pair_ref, ...), custom_call_target="tpu_custom_call" | custom-call | flops 115964116992 | bytes 201326592 | tf_op jit(solution)/shard_map/feed_forward/pallas_call | solution.py:480
  1063.7 48.5 %convolution_convert_fusion.2 = bf16[3072,768]{1,0:T(8,128)(2,1)} fusion(bf16[8192,3072]{1,0:T(8,128)(2,1)} %bitcast.273, bf16[8192,768]{1,0:T(8,128)(2,1)} %get-tuple-element.34), kind=kOutput, calls=%fused_computation.14 | convolution fusion | flops 38657064960 | bytes 67633152 | tf_op jit(solution)/shard_map/dot_general | solution.py:36
  1112.2 237.2 %shard_map.324 = f32[256,3072]{1,0:T(8,128)} custom-call(bf16[32,256,3072]{2,1,0:T(8,128)(2,1)} %bitcast.274), custom_call_target="tpu_custom_call" | custom-call | tf_op jit(solution)/shard_map/pallas_call | solution.py:434
  1349.5 29.3 %fusion.120 = f32[384,3072]{1,0:T(8,128)} fusion(bf16[8192,384]{1,0:T(8,128)(2,1)} %get-tuple-element.35, bf16[8192,3072]{1,0:T(8,128)(2,1)} %all-gather.2.cloned.1.call-done.cot_ref), kind=kOutput, calls=%fused_computation.238 | convolution fusion | flops 19327352832 | bytes 61341696 | tf_op jit(solution)/shard_map/dot_general | solution.py:36
  1380.2 2.8 multiply_add_fusion.1
  1383.0 15.5 fusion.60
  1398.5 2.3 slice.250
  1401.5 4.4 multiply_reduce_fusion.4
  1406.0 9.5 fusion.15
  1415.5 7.3 fusion.38
  1422.8 1.7 slice.254
  1425.1 4.6 fusion.64
  1429.7 3.6 multiply_reduce_fusion.7
  1436.2 2.9 convolution_bitcast_fusion.1
  1439.3 2.0 fusion.80
  1442.8 2.5 reduce-window.16
  1449.1 2.9 bitcast_add_fusion
  1453.2 9.4 multiply_reduce_fusion.3
  1462.6 2.1 fusion.20
  1464.8 2.1 fusion.19
  1467.0 2.5 fusion.18
  1471.6 2.8 fusion.59
  1480.3 24.2 %fusion.28 = (f32[3072]{0:T(1024)S(1)}, f32[256]{0:T(256)S(1)}, f32[256,3072]{1,0:T(8,128)}) fusion(bf16[256,3072]{1,0:T(8,128)(2,1)S(1)} %copy-done.14, f32[256]{0:T(256)S(1)} %copy-done.77, f32[3072]{0:T(1024)S(1)} %copy-done.52, bf16[256,8736]{0,1:T(8,128)(2,1)} %constant_dynamic-update-slice_fusion, bf16[3072,8736]{1,0:T(8,128)(2,1)} %bitcast.312), kind=kOutput, calls=%fused_computation.52 | convolution fusion | flops 13746041856 | bytes 62892032 | tf_op jit(solution)/shard_map/dot_general | solution.py:30
  1506.0 3.8 all-to-all-start.1
  1509.7 2.0 pad_maximum_fusion.1
  1512.3 12.7 convolution_convert_fusion.1
  1525.1 171.4 %shard_map.326 = f32[144,3072]{1,0:T(8,128)} custom-call(bf16[32,144,3072]{2,1,0:T(8,128)(2,1)} %bitcast.262), custom_call_target="tpu_custom_call" | custom-call | tf_op jit(solution)/shard_map/pallas_call | solution.py:434
  1696.4 2.5 slice.218
  1698.9 1.9 slice.221
  1700.8 29.8 %convolution_convert_fusion = bf16[3072,8736]{1,0:T(8,128)(2,1)} fusion(bf16[256,8736]{0,1:T(8,128)(2,1)} %constant_dynamic-update-slice_fusion, bf16[256,3072]{1,0:T(8,128)(2,1)S(1)} %copy-done.15, f32[3072]{0:T(1024)S(1)} %copy-done.52, f32[256]{0:T(256)S(1)} %copy-done.77), kind=kOutput, calls=%fused_computation | convolution fusion | flops 13770522624 | bytes 59732992 | tf_op jit(solution)/shard_map/dot_general | solution.py:36
  1730.7 351.7 %shard_map.325 = f32[96,8736]{1,0:T(8,128)} custom-call(bf16[32,96,8736]{2,1,0:T(8,128)(2,1)} %bitcast.261), custom_call_target="tpu_custom_call" | custom-call | tf_op jit(solution)/shard_map/pallas_call | solution.py:434
  2082.4 1.9 slice.219
  2085.8 6.0 fusion.27
  2092.6 1.7 fusion.116
  2100.5 10.2 reshape.439
  2110.8 12.3 fusion.114
  2123.1 2.7 copy_convert_fusion.1
  2125.8 5.4 copy.225
  2131.3 2.7 copy_convert_fusion
  2134.0 5.4 copy.226
  2139.5 112.6 %reduce-scatter.2.cloned.1.call-done = bf16[256,3072]{1,0:T(8,128)(2,1)} async-done(((bf16[8192,3072]{1,0:T(8,128)(2,1)}), bf16[256,3072]{1,0:T(8,128)(2,1)}) %reduce-scatter.2.cloned.1.call-update) | async-done | bytes 1572880 | tf_op jit(solution)/shard_map/reduce_scatter | solution.py:606
  2252.1 3.0 add_convert_fusion.1
  (367 shorter events, 55.6 us)
Async XLA Ops:
  7.2 890.8 %all-gather.2.cloned.1.call-start = ((), (), s32[]{:S(2)}) async-start(), calls=%async_computation.3 | async-start | bytes 51904512 | tf_op jit(solution)/shard_map/all_gather | solution.py:603
  401.6 4.9 copy-start.13
  401.6 496.4 %all-to-all-start = ((bf16[96,32,768]{2,0,1:T(8,128)(2,1)}), bf16[96,32,768]{2,0,1:T(8,128)(2,1)}, u32[]{:S(2)}, u32[]{:S(2)}) async-start(bf16[96,32,768]{2,0,1:T(8,128)(2,1)} %pad_maximum_fusion), calls=%async_computation | async-start | bytes 9437184 | tf_op jit(solution)/shard_map/all_to_all | solution.py:601
  405.5 1688.8 %all-reduce.27.cloned.1.call-start = ((), (), s32[]{:S(2)}) async-start(), calls=%async_computation.5 | async-start | bytes 196608 | tf_op jit(solution)/shard_map/psum | solution.py:645
  406.5 29.7 %copy-start.51 = (f32[3072]{0:T(1024)}, f32[3072]{0:T(1024)S(1)}, u32[]{:S(2)}) copy-start(f32[3072]{0:T(1024)S(1)} %reshape.441) | copy-start | bytes 36868
  406.9 29.3 %copy-start.76 = (f32[256]{0:T(256)}, f32[256]{0:T(256)S(1)}, u32[]{:S(2)}) copy-start(f32[256]{0:T(256)S(1)} %add_rsqrt_fusion.1) | copy-start | bytes 3076
  436.2 9.1 copy-start
  449.9 14.4 copy-start.96
  449.9 17.8 slice-start
  453.3 11.0 copy-start.67
  453.3 11.0 copy-start.69
  453.3 10.9 copy-start.71
  453.4 10.9 copy-start.73
  453.4 14.3 slice-start.1
  453.4 14.3 slice-start.2
  467.1 11.8 slice-start.12
  469.6 9.6 copy-start.91
  475.4 6.6 copy-start.37
  478.0 16.0 copy-start.35
  478.9 32.9 %copy-start.65 = (f32[3072]{0:T(1024)}, f32[3072]{0:T(1024)S(1)}, u32[]{:S(2)}) copy-start(f32[3072]{0:T(1024)S(1)} %reshape.442) | copy-start | bytes 36868
  479.9 5.3 copy-start.17
  480.0 5.9 copy-start.83
  485.2 8.8 copy-start.4
  485.2 8.8 copy-start.53
  485.9 411.5 %copy-start.55 = (f32[2,6,256]{2,1,0:T(8,128)}, f32[2,6,256]{2,1,0:T(8,128)S(1)}, u32[]{:S(2)}) copy-start(f32[2,6,256]{2,1,0:T(8,128)S(1)} %fusion.97) | copy-start | bytes 36868
  486.0 8.0 copy-start.48
  486.0 10.6 slice-start.3
  486.0 10.6 slice-start.4
  497.5 14.3 copy-start.16
  511.8 383.8 %copy-start.85 = (f32[256]{0:T(256)}, f32[256]{0:T(256)S(1)}, u32[]{:S(2)}) copy-start(f32[256]{0:T(256)S(1)} %add_rsqrt_fusion) | copy-start | bytes 3076
  515.0 380.6 %copy-start.103 = (pred[253]{0:T(512)(128)(4,1)S(1)}, pred[253]{0:T(512)(128)(4,1)}, u32[]{:S(2)}) copy-start(pred[253]{0:T(512)(128)(4,1)} %copy-done.102) | copy-start | bytes 763
  515.0 381.2 %copy-start.101 = (pred[254]{0:T(512)(128)(4,1)S(1)}, pred[254]{0:T(512)(128)(4,1)}, u32[]{:S(2)}) copy-start(pred[254]{0:T(512)(128)(4,1)} %copy-done.100) | copy-start | bytes 766
  1349.4 29.3 %copy-start.2 = (f32[256,3072]{1,0:T(8,128)S(1)}, f32[256,3072]{1,0:T(8,128)}, u32[]{:S(2)}) copy-start(f32[256,3072]{1,0:T(8,128)} %copy-done.1) | copy-start | bytes 9437188
  1349.4 29.3 %copy-start.11 = (f32[256,3072]{1,0:T(8,128)S(1)}, f32[256,3072]{1,0:T(8,128)}, u32[]{:S(2)}) copy-start(f32[256,3072]{1,0:T(8,128)} %shard_map.324) | copy-start | bytes 9437188
  1349.4 29.3 %copy-start.66 = (f32[3072]{0:T(1024)S(1)}, f32[3072]{0:T(1024)}, u32[]{:S(2)}) copy-start(f32[3072]{0:T(1024)} %copy-done.65) | copy-start | bytes 36868
  1349.5 29.3 %copy-start.86 = (f32[256]{0:T(256)S(1)}, f32[256]{0:T(256)}, u32[]{:S(2)}) copy-start(f32[256]{0:T(256)} %copy-done.85) | copy-start | bytes 3076
  1380.2 20.6 slice-start.6
  1383.0 17.8 slice-start.7
  1383.0 17.8 slice-start.8
  1401.5 4.4 copy-start.62
  1401.5 4.4 copy-start.79
  1401.5 4.5 copy-start.84
  1405.9 9.5 copy-start.20
  1415.5 9.0 copy-start.36
  1415.5 9.0 copy-start.54
  1415.5 9.0 copy-start.56
  1425.1 4.6 copy-start.49
  1425.1 4.6 copy-start.81
  1439.1 6.4 copy-start.38
  1439.3 6.2 copy-start.40
  1441.3 5.3 copy-start.42
  1441.3 5.3 copy-start.44
  1442.8 5.2 copy-start.82
  1453.2 9.4 copy-start.74
  1453.2 9.4 copy-start.106
  1464.8 6.1 slice-start.9
  1464.8 6.1 slice-start.10
  1474.4 5.8 copy-start.14
  1474.4 5.8 copy-start.52
  1474.4 5.8 copy-start.77
  1505.2 746.9 %reduce-scatter.2.cloned.1.call-start = ((), (), s32[]{:S(2)}) async-start(), calls=%async_computation.4 | async-start | bytes 51904512 | tf_op jit(solution)/shard_map/reduce_scatter | solution.py:606
  1506.0 594.6 %all-to-all-start.1 = ((bf16[32,96,768]{2,1,0:T(8,128)(2,1)}), bf16[32,96,768]{2,1,0:T(8,128)(2,1)}, u32[]{:S(2)}, u32[]{:S(2)}) async-start(bf16[32,96,768]{2,1,0:T(8,128)(2,1)} %bitcast.288), calls=%async_computation.2 | async-start | bytes 9437184 | tf_op jit(solution)/shard_map/all_to_all | solution.py:611
  2085.8 6.0 copy-start.19
  2134.0 118.1 %copy-start.3 = (f32[256,3072]{1,0:T(8,128)S(1)}, f32[256,3072]{1,0:T(8,128)}, u32[]{:S(2)}) copy-start(f32[256,3072]{1,0:T(8,128)} %copy-done.1) | copy-start | bytes 9437188
  (62 other events, 177.8 us)
Sparse Core Ops, SparseCore 0:
  396.7 488.4 all-gather.1
  1505.3 193.4 all-reduce.26
  1705.2 546.7 reduce-scatter.1
